TPU v7x, 64 devices: a 2x2x8 block of a 4x4x8 slice. The times are simulated.
64 devices in a mesh: dp: 4 (over x, y), wg: 16 (over z, core).
Axes of the slice: x: 2, y: 2, z: 8, core: 2. Of those that a mesh axis runs over, the one named last changes fastest.
The devices are a block of a 4x4x8 slice.
Arguments:
- x: bfloat16 [128, 128, 1024], P(('dp', 'wg')), parts along dimension 0
- positions: int32 [512], P('dp'), parts along dimension 0
- prompt_len: int32 [128], P(('dp', 'wg')), parts along dimension 0
- ln_attn: bfloat16 [2, 2, 1024], P(None, None, 'wg')
- ln_mlp: bfloat16 [2, 2, 1024], P(None, None, 'wg')
- w_qkv: bfloat16 [2, 1024, 3072], P(None, None, 'wg')
- w_out: bfloat16 [2, 16, 64, 1024], P(None, None, None, 'wg')
- w_up: bfloat16 [2, 1024, 4096], P(None, None, 'wg')
- w_down: bfloat16 [2, 4096, 1024], P(None, None, 'wg')
Outputs:
- output 1: bfloat16 [128, 128, 1024], P(('dp', 'wg')), parts along dimension 0
- output 2: bfloat16 [2, 128, 128, 16, 64], P(None, ('dp', 'wg')), parts along dimension 1
- output 3: bfloat16 [2, 128, 128, 16, 64], P(None, ('dp', 'wg')), parts along dimension 1
There are 4 independent parts. A program takes and returns all parts, laid end to end along the dimension named above; an argument that names none is the same for every part.
All inputs are finite; a program needn't handle non-finite values.
Results may differ from a plain program's by a relative error of at most 0.0119992.
Values are sent between devices in bfloat16 or wider.
A program may use at most 768 MiB of HBM per device.

v0:
```python
import jax
import jax.numpy as jnp
from jax import lax
from jax.sharding import PartitionSpec as P

EPSILON = 1e-5
ROPE_BASE = 10000.0


def layer_norm(tok_rows, norm_params):
    rows_f32 = tok_rows.astype(jnp.float32)
    row_mean = jnp.mean(rows_f32, axis=-1, keepdims=True)
    centered = rows_f32 - row_mean
    row_var = jnp.mean(centered * centered, axis=-1, keepdims=True)
    normed = centered * lax.rsqrt(row_var + EPSILON)
    return (normed * norm_params[0].astype(jnp.float32) + norm_params[1].astype(jnp.float32)).astype(jnp.bfloat16)


def rotary_tables(pos_rows, head_dim):
    half_dim = head_dim // 2
    inv_freq = ROPE_BASE ** (-jnp.arange(half_dim, dtype=jnp.float32) * 2.0 / head_dim)
    angles = pos_rows.astype(jnp.float32)[..., None] * inv_freq
    return jnp.cos(angles), jnp.sin(angles)


def apply_rotary(vec, cos_table, sin_table):
    half_dim = vec.shape[-1] // 2
    vec_f32 = vec.astype(jnp.float32)
    first_half = vec_f32[..., :half_dim]
    second_half = vec_f32[..., half_dim:]
    return jnp.concatenate([first_half * cos_table - second_half * sin_table, second_half * cos_table + first_half * sin_table], axis=-1).astype(jnp.bfloat16)


def attention(qkv_rows, prompt_len, cos_table, sin_table, kv_heads, head_dim):
    num_prompts, seq_len = qkv_rows.shape[0], qkv_rows.shape[1]
    grouped = qkv_rows.reshape(num_prompts, seq_len, kv_heads, -1, head_dim)
    q_per = grouped.shape[3] - 2
    query_rot = apply_rotary(grouped[:, :, :, :q_per, :], cos_table[:, :, None, None, :], sin_table[:, :, None, None, :])
    key_rot = apply_rotary(grouped[:, :, :, q_per, :], cos_table[:, :, None, :], sin_table[:, :, None, :])
    value_rows = grouped[:, :, :, q_per + 1, :]
    scores = jnp.einsum('bqgph,bkgh->bgpqk', query_rot, key_rot, preferred_element_type=jnp.float32) * head_dim ** -0.5
    q_index = jnp.arange(seq_len)[:, None]
    k_index = jnp.arange(seq_len)[None, :]
    allowed = (k_index <= q_index)[None] & (k_index[None] < prompt_len[:, None, None])
    scores = jnp.where(allowed[:, None, None], scores, -1e30)
    prob_bf16 = jax.nn.softmax(scores, axis=-1).astype(jnp.bfloat16)
    context = jnp.einsum('bgpqk,bkgh->bqgph', prob_bf16, value_rows, preferred_element_type=jnp.float32).astype(jnp.bfloat16)
    return context, key_rot, value_rows


def decoder_layer(x, prompt_len, cos_table, sin_table, ln_a, ln_m, w_qkv, w_out, w_up, w_down):
    num_heads, head_dim = w_out.shape[0], w_out.shape[1]
    kv_heads = (w_qkv.shape[1] // head_dim - num_heads) // 2
    h_attn = layer_norm(x, ln_a)
    h_mlp = layer_norm(x, ln_m)
    qkv_rows = jnp.einsum('bsd,df->bsf', h_attn, w_qkv, preferred_element_type=jnp.float32).astype(jnp.bfloat16)
    context, key_rot, value_rows = attention(qkv_rows, prompt_len, cos_table, sin_table, kv_heads, head_dim)
    w_out_grouped = w_out.reshape(kv_heads, num_heads // kv_heads, head_dim, -1)
    attn_out = jnp.einsum('bsgph,gphd->bsd', context, w_out_grouped, preferred_element_type=jnp.float32)
    hidden = jax.nn.gelu(jnp.einsum('bsd,df->bsf', h_mlp, w_up, preferred_element_type=jnp.float32), approximate=False).astype(jnp.bfloat16)
    mlp_out = jnp.einsum('bsf,fd->bsd', hidden, w_down, preferred_element_type=jnp.float32)
    new_rows = (x.astype(jnp.float32) + attn_out + mlp_out).astype(jnp.bfloat16)
    return new_rows, key_rot, value_rows


def solution(mesh):
    batch_spec = P(('dp', 'wg'))
    col_spec = P(None, None, 'wg')
    out_spec = P(None, None, None, 'wg')
    cache_spec = P(None, ('dp', 'wg'))

    def local_program(x, positions, prompt_len, ln_attn, ln_mlp, w_qkv, w_out, w_up, w_down):
        cos_table, sin_table = rotary_tables(positions, w_out.shape[2])
        hidden_rows = x
        key_list = []
        value_list = []
        for layer_idx in range(w_qkv.shape[0]):
            ln_a = lax.all_gather(ln_attn[layer_idx], 'wg', axis=1, tiled=True)
            ln_m = lax.all_gather(ln_mlp[layer_idx], 'wg', axis=1, tiled=True)
            qkv_full = lax.all_gather(w_qkv[layer_idx], 'wg', axis=1, tiled=True)
            out_full = lax.all_gather(w_out[layer_idx], 'wg', axis=2, tiled=True)
            up_full = lax.all_gather(w_up[layer_idx], 'wg', axis=1, tiled=True)
            down_full = lax.all_gather(w_down[layer_idx], 'wg', axis=1, tiled=True)
            hidden_rows, key_rot, value_rows = decoder_layer(hidden_rows, prompt_len, cos_table[None], sin_table[None], ln_a, ln_m, qkv_full, out_full, up_full, down_full)
            key_list.append(key_rot)
            value_list.append(value_rows)
        return hidden_rows, jnp.stack(key_list), jnp.stack(value_list)

    return jax.shard_map(local_program, mesh=mesh, in_specs=(batch_spec, P('dp'), batch_spec, col_spec, col_spec, col_spec, out_spec, col_spec, col_spec), out_specs=(batch_spec, cache_spec, cache_spec), check_vma=False)
```

profile of v0, /device:TPU:21, one launch (start us, length us, event | category | flops | bytes accessed | tf_op | source)
XLA Modules:
  0.0 432.3 jit_solution(4220904343583802330)
XLA Ops:
  10.7 2.0 fusion.294
  18.0 25.5 %all-gather = bf16[1,2,1024]{1,0,2:T(2,128)(2,1)S(1)} all-gather(bf16[1,2,64]{1,0,2:T(2,128)(2,1)S(1)} %copy.83), channel_id=2, replica_groups=mesh['dp'=4,'wg'=16] {'wg'}, dimensions={2}, use_global_device_ids=true | all-gather | bytes 4352 | tf_op jit(solution)/shard_map/all_gather | solution.py:78
  43.5 17.0 %all-gather.3 = bf16[1,2,1024]{1,0,2:T(2,128)(2,1)S(1)} all-gather(bf16[1,2,64]{1,0,2:T(2,128)(2,1)S(1)} %copy.88), channel_id=5, replica_groups=mesh['dp'=4,'wg'=16] {'wg'}, dimensions={2}, use_global_device_ids=true | all-gather | bytes 4352 | tf_op jit(solution)/shard_map/all_gather | solution.py:79
  60.5 18.7 %all-gather.6 = bf16[1,2,1024]{1,0,2:T(2,128)(2,1)S(1)} all-gather(bf16[1,2,64]{1,0,2:T(2,128)(2,1)S(1)} %copy.89), channel_id=8, replica_groups=mesh['dp'=4,'wg'=16] {'wg'}, dimensions={2}, use_global_device_ids=true | all-gather | bytes 4352 | tf_op jit(solution)/shard_map/all_gather | solution.py:78
  79.2 17.7 %all-gather.9 = bf16[1,2,1024]{1,0,2:T(2,128)(2,1)S(1)} all-gather(bf16[1,2,64]{1,0,2:T(2,128)(2,1)S(1)} %copy.94), channel_id=11, replica_groups=mesh['dp'=4,'wg'=16] {'wg'}, dimensions={2}, use_global_device_ids=true | all-gather | bytes 4352 | tf_op jit(solution)/shard_map/all_gather | solution.py:79
  97.7 7.3 %fusion.187 = (f32[1024]{0:T(1024)S(1)}, f32[1024]{0:T(1024)S(1)}) fusion(bf16[1,2,1024]{1,0,2:T(2,128)(2,1)S(1)} %all-gather), kind=kLoop, calls=%fused_computation.202 | loop fusion | flops 2048 | bytes 12288 | tf_op jit(solution)/shard_map/convert_element_type | solution.py:16
  105.1 7.3 %fusion.183 = (f32[1024]{0:T(1024)S(1)}, f32[1024]{0:T(1024)S(1)}) fusion(bf16[1,2,1024]{1,0,2:T(2,128)(2,1)S(1)} %all-gather.3), kind=kLoop, calls=%fused_computation.194 | loop fusion | flops 2048 | bytes 12288 | tf_op jit(solution)/shard_map/convert_element_type | solution.py:16
  112.4 7.6 %fusion.181 = (f32[1024]{0:T(1024)S(1)}, f32[1024]{0:T(1024)S(1)}) fusion(bf16[1,2,1024]{1,0,2:T(2,128)(2,1)S(1)} %all-gather.6), kind=kLoop, calls=%fused_computation.190 | loop fusion | flops 2048 | bytes 12288 | tf_op jit(solution)/shard_map/convert_element_type | solution.py:16
  120.0 7.3 %fusion.177 = (f32[1024]{0:T(1024)S(1)}, f32[1024]{0:T(1024)S(1)}) fusion(bf16[1,2,1024]{1,0,2:T(2,128)(2,1)S(1)} %all-gather.9), kind=kLoop, calls=%fused_computation.182 | loop fusion | flops 2048 | bytes 12288 | tf_op jit(solution)/shard_map/convert_element_type | solution.py:16
  127.4 5.9 %copy.65 = bf16[1,16,64,1024]{3,2,1,0:T(8,128)(2,1)} copy(bf16[1,16,64,1024]{2,1,0,3:T(8,128)(2,1)} %all-gather.23.cloned.1.call-done) | data formatting | bytes 4194304 | tf_op jit(solution)/shard_map/all_gather | solution.py:81
  133.3 5.5 %copy.76 = bf16[1,16,64,1024]{3,2,1,0:T(8,128)(2,1)} copy(bf16[1,16,64,1024]{2,1,0,3:T(8,128)(2,1)} %all-gather.31.cloned.1.call-done) | data formatting | bytes 4194304 | tf_op jit(solution)/shard_map/all_gather | solution.py:81
  139.6 5.8 %fusion.30 = bf16[2,128,3072]{2,1,0:T(8,128)(2,1)} fusion(bf16[1,1024,3072]{1,2,0:T(8,128)(2,1)} %all-gather.21.cloned.1.call-done, bf16[2,128,1024]{2,1,0:T(8,128)(2,1)S(1)} %copy-done.2, f32[1024]{0:T(1024)S(1)} %get-tuple-element.14, f32[1024]{0:T(1024)S(1)} %get-tuple-element.13, f32[2,128]{1,0:T(2,128)S(1)} %add_rsqrt_fusion.1, ...), kind=kOutput, calls=%fused_computation.55 | convolution fusion | flops 1612972032 | bytes 8398848 | tf_op jit(solution)/shard_map/bsd,df->bsf/dot_general | solution.py:56
  150.2 4.3 convert_add_fusion.1
  154.4 46.3 %all-gather.25.cloned.1.call-done = bf16[1,1024,4096]{2,1,0:T(8,128)(2,1)} async-done(((bf16[1,1024,256]{2,1,0:T(8,128)(2,1)}), bf16[1,1024,4096]{2,1,0:T(8,128)(2,1)}) %all-gather.25.cloned.1.call-update) | async-done | bytes 8388624 | tf_op jit(solution)/shard_map/all_gather | solution.py:82
  200.8 10.2 %fusion.166 = (u8[128,4096]{1,0:T(8,128)(4,1)}, u8[128,4096]{1,0:T(8,128)(4,1)}, f32[2,128,4096]{2,1,0:T(8,128)}) fusion(bf16[1,1024,4096]{2,1,0:T(8,128)(2,1)} %all-gather.25.cloned.1.call-done, bf16[2,128,1024]{2,1,0:T(8,128)(2,1)S(1)} %copy-done.2, f32[1024]{0:T(1024)S(1)} %get-tuple-element.12, f32[1024]{0:T(1024)S(1)} %get-tuple-element.11, ...), kind=kOutput, calls=%fused_computation.173 | convolution fusion | flops 2161639424 | bytes 14166016 | tf_op jit(solution)/shard_map/bsd,df->bsf/dot_general | solution.py:60
  210.9 42.5 %all-gather.27.cloned.1.call-done = bf16[1,4096,1024]{1,2,0:T(8,128)(2,1)} async-done(((bf16[1,4096,64]{1,2,0:T(8,128)(2,1)}), bf16[1,4096,1024]{1,2,0:T(8,128)(2,1)}) %all-gather.27.cloned.1.call-update) | async-done | bytes 8388624 | tf_op jit(solution)/shard_map/all_gather | solution.py:83
  253.4 14.1 %convert_reduce_fusion = (f32[2,128]{1,0:T(2,128)S(1)}, bf16[2,128,1024]{2,1,0:T(8,128)(2,1)S(1)}) fusion(f32[2,128,1024]{2,1,0:T(8,128)S(1)} %copy-done.11, bf16[1,4096,1024]{1,2,0:T(8,128)(2,1)} %all-gather.27.cloned.1.call-done, f32[2,128,4096]{2,1,0:T(8,128)} %get-tuple-element.45, u8[128,4096]{1,0:T(8,128)(4,1)} %get-tuple-element.6, ...), kind=kOutput, calls=%fused_computation.133 | convolution fusion | flops 2221932288 | bytes 15205376 | tf_op jit(solution)/shard_map/bsf,fd->bsd/dot_general | solution.py:61
  267.8 28.6 %all-gather.29.cloned.1.call-done = bf16[1,1024,3072]{1,2,0:T(8,128)(2,1)} async-done(((bf16[1,1024,192]{1,2,0:T(8,128)(2,1)}), bf16[1,1024,3072]{1,2,0:T(8,128)(2,1)}) %all-gather.29.cloned.1.call-update) | async-done | bytes 6291472 | tf_op jit(solution)/shard_map/all_gather | solution.py:80
  296.4 5.8 %fusion.33 = bf16[2,128,3072]{2,1,0:T(8,128)(2,1)} fusion(bf16[1,1024,3072]{1,2,0:T(8,128)(2,1)} %all-gather.29.cloned.1.call-done, bf16[2,128,1024]{2,1,0:T(8,128)(2,1)S(1)} %get-tuple-element.47, f32[1024]{0:T(1024)S(1)} %get-tuple-element.10, f32[1024]{0:T(1024)S(1)} %get-tuple-element.9, f32[2,128]{1,0:T(2,128)S(1)} %add_rsqrt_fusion, ...), kind=kOutput, calls=%fused_computation.56 | convolution fusion | flops 1612972032 | bytes 8398848 | tf_op jit(solution)/shard_map/bsd,df->bsf/dot_general | solution.py:56
  308.6 4.3 convert_add_fusion
  312.8 44.9 %all-gather.33.cloned.1.call-done = bf16[1,1024,4096]{2,1,0:T(8,128)(2,1)} async-done(((bf16[1,1024,256]{2,1,0:T(8,128)(2,1)}), bf16[1,1024,4096]{2,1,0:T(8,128)(2,1)}) %all-gather.33.cloned.1.call-update) | async-done | bytes 8388624 | tf_op jit(solution)/shard_map/all_gather | solution.py:82
  357.7 9.0 %fusion.167 = (u8[128,4096]{1,0:T(8,128)(4,1)S(1)}, u8[128,4096]{1,0:T(8,128)(4,1)S(1)}, f32[2,128,4096]{2,1,0:T(8,128)}) fusion(bf16[1,1024,4096]{2,1,0:T(8,128)(2,1)} %all-gather.33.cloned.1.call-done, bf16[2,128,1024]{2,1,0:T(8,128)(2,1)S(1)} %copy-done.6, f32[1024]{0:T(1024)S(1)} %get-tuple-element.8, f32[1024]{0:T(1024)S(1)} %get-tuple-element.7, ...), kind=kOutput, calls=%fused_computation.174 | convolution fusion | flops 2161639424 | bytes 14166016 | tf_op jit(solution)/shard_map/bsd,df->bsf/dot_general | solution.py:60
  366.7 43.8 %all-gather.35.cloned.1.call-done = bf16[1,4096,1024]{1,2,0:T(8,128)(2,1)} async-done(((bf16[1,4096,64]{1,2,0:T(8,128)(2,1)}), bf16[1,4096,1024]{1,2,0:T(8,128)(2,1)}) %all-gather.35.cloned.1.call-update) | async-done | bytes 8388624 | tf_op jit(solution)/shard_map/all_gather | solution.py:83
  410.6 14.7 %fusion.126 = bf16[2,128,1024]{2,1,0:T(8,128)(2,1)} fusion(f32[2,128,1024]{2,1,0:T(8,128)S(1)} %copy-done.12, bf16[1,4096,1024]{1,2,0:T(8,128)(2,1)} %all-gather.35.cloned.1.call-done, f32[2,128,4096]{2,1,0:T(8,128)} %get-tuple-element.50, u8[128,4096]{1,0:T(8,128)(4,1)S(1)} %get-tuple-element.4, u8[128,4096]{1,0:T(8,128)(4,1)S(1)} %get-tuple-element.3), kind=kOutput, calls=%fused_computation.143 | convolution fusion | flops 2221408256 | bytes 15204352 | tf_op jit(solution)/shard_map/bsf,fd->bsd/dot_general | solution.py:61
  (82 shorter events, 21.3 us)
Async XLA Ops:
  7.2 5.7 %copy-start.3 = (bf16[2,1024,256]{2,1,0:T(8,128)(2,1)S(1)}, bf16[2,1024,256]{2,1,0:T(8,128)(2,1)}, u32[]{:S(2)}) copy-start(bf16[2,1024,256]{2,1,0:T(8,128)(2,1)} %param.16) | copy-start | bytes 3145732
  7.2 6.9 %copy-start.4 = (bf16[2,4096,64]{1,2,0:T(8,128)(2,1)S(1)}, bf16[2,4096,64]{1,2,0:T(8,128)(2,1)}, u32[]{:S(2)}) copy-start(bf16[2,4096,64]{1,2,0:T(8,128)(2,1)} %param.17) | copy-start | bytes 3145732
  7.2 120.2 %all-gather.23.cloned.1.call-start = ((), (), s32[]{:S(2)}) async-start(), calls=%async_computation.1 | async-start | bytes 4456448 | tf_op jit(solution)/shard_map/all_gather | solution.py:81
  9.5 123.9 %all-gather.31.cloned.1.call-start = ((), (), s32[]{:S(2)}) async-start(), calls=%async_computation.5 | async-start | bytes 4456448 | tf_op jit(solution)/shard_map/all_gather | solution.py:81
  10.6 6.9 %copy-start.7 = (bf16[2,2,64]{2,1,0:T(2,128)(2,1)S(1)}, bf16[2,2,64]{2,1,0:T(2,128)(2,1)}, u32[]{:S(2)}) copy-start(bf16[2,2,64]{2,1,0:T(2,128)(2,1)} %param.12) | copy-start | bytes 1540
  10.6 7.0 %copy-start.9 = (s32[128]{0:T(128)S(1)}, s32[128]{0:T(128)}, u32[]{:S(2)}) copy-start(s32[128]{0:T(128)} %param.10) | copy-start | bytes 1540
  10.6 7.0 %copy-start.8 = (bf16[2,2,64]{2,1,0:T(2,128)(2,1)S(1)}, bf16[2,2,64]{2,1,0:T(2,128)(2,1)}, u32[]{:S(2)}) copy-start(bf16[2,2,64]{2,1,0:T(2,128)(2,1)} %param.13) | copy-start | bytes 1540
  10.6 129.0 %all-gather.21.cloned.1.call-start = ((), (), s32[]{:S(2)}) async-start(), calls=%async_computation | async-start | bytes 6684672 | tf_op jit(solution)/shard_map/all_gather | solution.py:80
  12.8 84.2 %copy-start.2 = (bf16[2,128,1024]{2,1,0:T(8,128)(2,1)S(1)}, bf16[2,128,1024]{2,1,0:T(8,128)(2,1)}, u32[]{:S(2)}) copy-start(bf16[2,128,1024]{2,1,0:T(8,128)(2,1)} %param.9) | copy-start | bytes 1572868
  12.8 188.0 %all-gather.25.cloned.1.call-start = ((), (), s32[]{:S(2)}) async-start(), calls=%async_computation.2 | async-start | bytes 8912896 | tf_op jit(solution)/shard_map/all_gather | solution.py:82
  13.9 83.5 %copy-start.10 = (s32[2]{0:T(128)S(1)}, s32[2]{0:T(128)}, u32[]{:S(2)}) copy-start(s32[2]{0:T(128)} %param.11) | copy-start | bytes 28
  14.0 239.4 %all-gather.27.cloned.1.call-start = ((), (), s32[]{:S(2)}) async-start(), calls=%async_computation.3 | async-start | bytes 8912896 | tf_op jit(solution)/shard_map/all_gather | solution.py:83
  15.2 281.2 %all-gather.29.cloned.1.call-start = ((), (), s32[]{:S(2)}) async-start(), calls=%async_computation.4 | async-start | bytes 6684672 | tf_op jit(solution)/shard_map/all_gather | solution.py:80
  15.8 341.9 %all-gather.33.cloned.1.call-start = ((), (), s32[]{:S(2)}) async-start(), calls=%async_computation.6 | async-start | bytes 8912896 | tf_op jit(solution)/shard_map/all_gather | solution.py:82
  16.6 393.9 %all-gather.35.cloned.1.call-start = ((), (), s32[]{:S(2)}) async-start(), calls=%async_computation.7 | async-start | bytes 8912896 | tf_op jit(solution)/shard_map/all_gather | solution.py:83
  148.4 1.4 copy-start.1
  200.8 52.7 %copy-start.11 = (f32[2,128,1024]{2,1,0:T(8,128)S(1)}, f32[2,128,1024]{2,1,0:T(8,128)}, u32[]{:S(2)}) copy-start(f32[2,128,1024]{2,1,0:T(8,128)} %convert_add_fusion.1) | copy-start | bytes 3145732
  267.5 28.9 %copy-start.5 = (bf16[2,128,1024]{2,1,0:T(8,128)(2,1)}, bf16[2,128,1024]{2,1,0:T(8,128)(2,1)S(1)}, u32[]{:S(2)}) copy-start(bf16[2,128,1024]{2,1,0:T(8,128)(2,1)S(1)} %get-tuple-element.47) | copy-start | bytes 1572868
  306.1 2.5 copy-start.6
  306.8 1.3 copy-start
  357.7 52.9 %copy-start.12 = (f32[2,128,1024]{2,1,0:T(8,128)S(1)}, f32[2,128,1024]{2,1,0:T(8,128)}, u32[]{:S(2)}) copy-start(f32[2,128,1024]{2,1,0:T(8,128)} %convert_add_fusion) | copy-start | bytes 3145732
Sparse Core Ops, SparseCore 0:
  9.7 45.7 all-gather.22
  57.1 38.6 all-gather.30
  98.0 41.5 all-gather.20
  141.0 59.7 all-gather.24
  202.8 50.5 all-gather.26
  254.9 41.4 all-gather.28
  298.0 59.7 all-gather.32
  359.9 50.6 all-gather.34
where the time goes:
time: 436 us; the launch traced here: 432 us
  waiting for transfers between devices  209 us (48%)
  blocking collectives  78.9 us (18%)
  matrix products  69.2 us (16%)
  other arithmetic  34 us (8%)
  local copies, waits for them, and re-layouts  25.6 us (6%)
  between operations  14.7 us (3%)
    all_gather x2, waiting for transfers between devices, local_program(): up_full = lax.all_gather(w_up[layer_idx], 'wg', axis=1, tiled=True)  91.2 us
    all_gather x2, waiting for transfers between devices, local_program(): down_full = lax.all_gather(w_down[layer_idx], 'wg', axis=1, tiled=True)  86.3 us
    all_gather x2, blocking collectives, local_program(): ln_a = lax.all_gather(ln_attn[layer_idx], 'wg', axis=1, tiled=True)  44.2 us
    all_gather x2, blocking collectives, local_program(): ln_m = lax.all_gather(ln_mlp[layer_idx], 'wg', axis=1, tiled=True)  34.7 us
    convert_element_type x4, other arithmetic, layer_norm(): norm_params[0].astype(jnp.float32)  29.6 us
    all_gather x2, waiting for transfers between devices, local_program(): qkv_full = lax.all_gather(w_qkv[layer_idx], 'wg', axis=1, tiled=True)  29.4 us
    dot_general x2, matrix products, decoder_layer(): jnp.einsum('bsf,fd->bsd', hidden, w_down, preferred_element_type=jnp.floa...  28.7 us
    dot_general x2, matrix products, decoder_layer(): jnp.einsum('bsd,df->bsf', h_mlp, w_up, preferred_element_type=jnp.float32)  19.2 us
  transfers between devices with their start and end apart: 8, of which 6 were waited for; matrix products, arithmetic and copies ran while one was open for 25% of the time, Pallas kernels for 0%

commit v1 on v0

v1 whole, which is shorter than its diff:
```python
import functools
import math

import jax
import jax.numpy as jnp
from jax import lax
from jax.experimental import pallas as pl
from jax.experimental.pallas import tpu as pltpu
from jax.sharding import PartitionSpec as P

EPSILON = 1e-5
ROPE_BASE = 10000.0
MESH = pl.DeviceIdType.MESH
F32 = jnp.float32
BF16 = jnp.bfloat16
QUARTERS = 4
UNITS = 3


def kernel(
    cols,
    chips,
    layers,
    x_hbm,
    cos_ref,
    sin_ref,
    len_ref,
    ln_ref,
    qkv_hbm,
    up_hbm,
    out_hbm,
    down_hbm,
    y_ref,
    k_ref,
    v_ref,
    buf_q,
    buf_u,
    buf_d,
    up_nat,
    out_nat,
    x_nat,
    x_t,
    a_t,
    m_t,
    ctx_t,
    hid_t,
    acc,
    ln_all,
    z_recv,
    xy_recv,
    sib_recv,
    z_send,
    xy_send,
    sib_send,
    ln_recv,
    ln_send,
    ln_sib,
    load_sem,
):
    half = chips // 2
    d_me = lax.axis_index("dp")
    w_me = lax.axis_index("wg")
    z, c = w_me // 2, w_me % 2
    x_pos, y_pos = d_me // cols, d_me % cols
    px, py = x_pos % 2, y_pos % 2
    dev_z = ({"wg": lax.rem(z + 1, chips) * 2 + c}, {"wg": lax.rem(z + chips - 1, chips) * 2 + c})
    dev_xy = ({"dp": d_me + cols * (1 - 2 * px)}, {"dp": d_me + 1 - 2 * py})
    dev_sib = {"wg": z * 2 + 1 - c}
    quarter_z = (px, 2 + py)
    quarter_xy = (1 - px, 3 - py)
    bufs = (buf_q, buf_u, buf_d)
    hops = ((half, half - 1), (half - 1, half))

    def chip_at(direction, h):
        return lax.rem(z + chips - h, chips) if direction == 0 else lax.rem(z + h, chips)

    def slot(chip, core, quarter):
        return (chip * 2 + core) * QUARTERS + quarter

    def remote(src, dst, send, recv, dev):
        return pltpu.make_async_remote_copy(
            src_ref=src, dst_ref=dst, send_sem=send, recv_sem=recv, device_id=dev, device_id_type=MESH
        )

    def z_copy(l, u, direction, s, h):
        ref = bufs[u].at[l, slot(chip_at(direction, h - 1), c, quarter_z[s])]
        return remote(ref, ref, z_send.at[l * UNITS + u, direction], z_recv.at[l * UNITS + u, direction * 2 + s, h - 1], dev_z[direction])

    def z_arrival(l, u, direction, s, h):
        ref = bufs[u].at[l, slot(chip_at(direction, h), c, quarter_z[s])]
        return remote(ref, ref, z_send.at[l * UNITS + u, direction], z_recv.at[l * UNITS + u, direction * 2 + s, h - 1], dev_z[direction])

    def source_index(direction, h):
        return (h - 1) * 2 + direction if h < half else chips - 2

    def xy_copy(l, u, direction, s, h, quarter):
        ref = bufs[u].at[l, slot(chip_at(direction, h), c, quarter)]
        return remote(ref, ref, xy_send.at[l * UNITS + u, s], xy_recv.at[l * UNITS + u, s, source_index(direction, h)], dev_xy[s])

    def sib_copy(l, u, chip, core, index):
        ref = bufs[u].at[l, pl.ds(slot(chip, core, 0), QUARTERS)]
        return remote(ref, ref, sib_send.at[l * UNITS + u], sib_recv.at[l * UNITS + u, index], dev_sib)

    def send_own(l, u, s):
        for direction in (0, 1):
            z_copy(l, u, direction, s, 1).start()

    def send_own_sib(l, u):
        sib_copy(l, u, z, c, chips - 1).start()

    def forward(l, u, h, s):
        for direction in (0, 1):
            if h > hops[direction][s]:
                continue
            z_arrival(l, u, direction, s, h).wait_recv()
            if h < hops[direction][s]:
                z_copy(l, u, direction, s, h + 1).start()
            xy_copy(l, u, direction, s, h, quarter_z[s]).start()

    def sources(h):
        return (0, 1) if h < half else (0,)

    def share_with_sibling(l, u, h):
        for direction in sources(h):
            for s in (0, 1):
                xy_copy(l, u, direction, s, h, quarter_xy[s]).wait_recv()
            sib_copy(l, u, chip_at(direction, h), c, source_index(direction, h)).start()

    def wait_sibling(l, u, h):
        for direction in sources(h):
            sib_copy(l, u, chip_at(direction, h), 1 - c, source_index(direction, h)).wait_recv()
        if h == half:
            sib_copy(l, u, z, 1 - c, chips - 1).wait_recv()

    def ln_hop(h):
        for direction in (0, 1):
            limit = half - direction
            if h > limit:
                continue
            if h > 0:
                ref = ln_all.at[c, chip_at(direction, h)]
                remote(ref, ref, ln_send.at[direction], ln_recv.at[direction, h - 1], dev_z[direction]).wait_recv()
            if h < limit:
                dst = ln_all.at[c, chip_at(direction, h)]
                src = ln_ref if h == 0 else dst
                remote(src, dst, ln_send.at[direction], ln_recv.at[direction, h], dev_z[direction]).start()

    def ln_share(core):
        return remote(ln_all.at[core], ln_all.at[core], ln_sib.at[0], ln_sib.at[1], dev_sib)


    def normalize(l):
        rows = x_t[...].reshape(-1, x_t.shape[-1]).astype(F32)
        centered = rows - jnp.mean(rows, axis=0, keepdims=True)
        var = jnp.mean(centered * centered, axis=0, keepdims=True)
        normed = centered * lax.rsqrt(var + EPSILON)
        params = ln_all[:, :, l].reshape(-1, 128).T
        step = x_t.shape[1]
        for w in range(2 * chips):
            block = normed[w * step : (w + 1) * step]
            base = ((w % 2) * chips + w // 2) * 8
            column = [params[:step, base + r : base + r + 1] for r in range(4)]
            a_t[w * step : (w + 1) * step, :] = (block * column[0] + column[1]).astype(BF16)
            m_t[w * step : (w + 1) * step, :] = (block * column[2] + column[3]).astype(BF16)

    def rotate(vec, cos, sin):
        first, second = vec[: cos.shape[0]].astype(F32), vec[cos.shape[0] :].astype(F32)
        return jnp.concatenate([first * cos - second * sin, second * cos + first * sin], axis=0).astype(BF16)

    def compute_qkv(l, chip):
        head_dim = k_ref.shape[3]
        seq = k_ref.shape[4]
        cos, sin = cos_ref[...], sin_ref[...]
        k_index = lax.broadcasted_iota(jnp.int32, (seq, seq), 0)
        q_index = lax.broadcasted_iota(jnp.int32, (seq, seq), 1)
        for core in (0, 1):
            head = chip * 2 + core
            share = buf_q[l, pl.ds(slot(chip, core, 0), QUARTERS)]
            share = share.reshape(-1, share.shape[-1])
            qkv = jnp.dot(share, a_t[...], preferred_element_type=F32).astype(BF16)
            for b in range(k_ref.shape[1]):
                cols_b = slice(b * seq, (b + 1) * seq)
                q_t = rotate(qkv[:head_dim, cols_b], cos, sin)
                k_t = rotate(qkv[head_dim : 2 * head_dim, cols_b], cos, sin)
                v_t = qkv[2 * head_dim :, cols_b]
                k_ref[l, b, head] = k_t
                v_ref[l, b, head] = v_t
                scores = jnp.dot(k_t.T, q_t, preferred_element_type=F32) * head_dim**-0.5
                allowed = (k_index <= q_index) & (k_index < len_ref[b])
                scores = jnp.where(allowed, scores, -1e30)
                top = jnp.max(scores, axis=0, keepdims=True)
                expo = jnp.exp(scores - top)
                prob = (expo * (1.0 / jnp.sum(expo, axis=0, keepdims=True))).astype(BF16)
                ctx_t[head, :, cols_b] = jnp.dot(v_t, prob, preferred_element_type=F32).astype(BF16)

    def compute_up(l, chip):
        up_rows = up_hbm.shape[2] // QUARTERS
        for core in (0, 1):
            share = buf_u[l, pl.ds(slot(chip, core, 0), QUARTERS), :up_rows, :]
            share = share.reshape(-1, share.shape[-1])
            pre = jnp.dot(share, m_t[...], preferred_element_type=F32)
            hid_t[chip * 2 + core] = (0.5 * pre * (1.0 + lax.erf(pre * 0.5**0.5))).astype(BF16)
        share = buf_u[l, pl.ds(slot(chip, 0, 0), 2 * QUARTERS), up_rows:, :]
        share = share.reshape(-1, share.shape[-1])
        ctx = ctx_t[...].reshape(-1, ctx_t.shape[-1])
        attn_out = jnp.dot(share, ctx, preferred_element_type=F32)
        acc[pl.ds(chip * 2, 2)] = attn_out.reshape((2,) + acc.shape[1:])

    def compute_down(l, chip):
        share = buf_d[l, pl.ds(slot(chip, 0, 0), 2 * QUARTERS)]
        share = share.reshape(-1, share.shape[-1])
        hidden = hid_t[...].reshape(-1, hid_t.shape[-1])
        mlp_out = jnp.dot(share, hidden, preferred_element_type=F32).reshape((2,) + acc.shape[1:])
        both = pl.ds(chip * 2, 2)
        x_t[both] = (x_t[both].astype(F32) + acc[both] + mlp_out).astype(BF16)

    computes = (compute_qkv, compute_up, compute_down)

    def compute(l, u, h):
        wait_sibling(l, u, h)
        if u == 0 and h == 1:

            @pl.when(l == 0)
            def _():
                ln_share(1 - c).wait_recv()

            normalize(l)

        @pl.loop(0, 2)
        def _(i):
            shift = chips - h + i * 2 * h if h < half else half + i * half
            computes[u](l, lax.rem(z + shift, chips))


    own = pl.ds(slot(z, c, 0), QUARTERS)
    loads = [pltpu.make_async_copy(qkv_hbm.at[l], buf_q.at[l, own], load_sem.at[l]) for l in range(layers)]
    loads += [pltpu.make_async_copy(down_hbm.at[l], buf_d.at[l, own], load_sem.at[layers + l]) for l in range(layers)]
    load_up = pltpu.make_async_copy(up_hbm, up_nat, load_sem.at[2 * layers])
    load_out = pltpu.make_async_copy(out_hbm, out_nat, load_sem.at[2 * layers + 1])
    load_x = pltpu.make_async_copy(x_hbm, x_nat, load_sem.at[2 * layers + 2])
    loads[0].start()
    load_x.start()
    load_up.start()
    load_out.start()
    for load in loads[1:]:
        load.start()

    barrier = pltpu.get_barrier_semaphore()
    neighbours = dev_z + dev_xy + (dev_sib,)
    for dev in neighbours:
        pl.semaphore_signal(barrier, inc=1, device_id=dev, device_id_type=MESH)
    ln_all[c, z] = ln_ref[...]
    loads[0].wait()
    pl.semaphore_wait(barrier, len(neighbours))

    ln_hop(0)
    send_own(0, 0, 0)
    send_own(0, 0, 1)
    send_own_sib(0, 0)
    load_x.wait()
    seq = x_hbm.shape[1]
    for b in range(x_hbm.shape[0]):
        x_t[:, :, b * seq : (b + 1) * seq] = x_nat[b].T.reshape(x_t.shape[0], x_t.shape[1], seq)
    ln_hop(1)
    load_up.wait()
    load_out.wait()
    up_rows = up_hbm.shape[2] // QUARTERS

    def place_up(l):
        up_t = up_nat[l].T
        buf_u[l, own, :up_rows, :] = up_t.reshape(QUARTERS, up_rows, up_t.shape[-1])
        out_t = out_nat[l].T
        buf_u[l, own, up_rows:, :] = out_t.reshape(QUARTERS, -1, out_t.shape[-1])

    place_up(0)


    order = [(u, h) for u in range(UNITS) for h in range(1, half + 1)]

    def back(n, k):
        return (order[n - k], 0) if n >= k else (order[n - k], -1)

    @pl.loop(0, layers)
    def _(l):
        first = l == 0

        def lagged(action, n, k):
            (u, h), offset = back(n, k)
            if offset == 0:
                action(l, u, h)
            else:

                @pl.when(l > 0)
                def _():
                    action(l - 1, u, h)

        for n, (u, h) in enumerate(order):
            if u == 0 and h <= 2:

                @pl.when(first)
                def _():
                    ln_hop(2 * h)

            forward(l, u, h, 0)
            if u == 0 and h == 1:

                @pl.when(first)
                def _():
                    ln_hop(3)

            forward(l, u, h, 1)
            if u == 0 and h == 2:

                @pl.when(first)
                def _():
                    ln_share(c).start()
                    for load in loads[1:]:
                        load.wait()
                    place_up(1)

            if h == half - 1:
                if u + 1 < UNITS:
                    for s in (0, 1):
                        send_own(l, u + 1, s)
                    send_own_sib(l, u + 1)
                else:

                    @pl.when(l + 1 < layers)
                    def _():
                        for s in (0, 1):
                            send_own(l + 1, 0, s)
                        send_own_sib(l + 1, 0)

            lagged(share_with_sibling, n, 1)
            lagged(compute, n, 2)

    last = layers - 1
    share_with_sibling(last, UNITS - 1, half)
    compute(last, UNITS - 1, half - 1)
    compute(last, UNITS - 1, half)
    y_t = x_t[...].reshape(-1, x_t.shape[-1])
    for b in range(y_ref.shape[0]):
        y_ref[b] = y_t[:, b * seq : (b + 1) * seq].T

    ref = ln_all.at[c]
    for direction in (0, 1):
        src = ref.at[pl.ds(0, half - direction)]
        remote(src, src, ln_send.at[direction], ln_sib.at[1], dev_z[direction]).wait_send()
    ln_share(c).wait_send()

    @pl.loop(0, layers)
    def _(l):
        for u in range(UNITS):
            sent = bufs[u].at[l, pl.ds(0, chips - 1)]
            for i in (0, 1):
                remote(sent, sent, z_send.at[l * UNITS + u, i], ln_sib.at[1], dev_z[i]).wait_send()
                remote(sent, sent, xy_send.at[l * UNITS + u, i], ln_sib.at[1], dev_xy[i]).wait_send()
            sent = bufs[u].at[l, pl.ds(0, chips * QUARTERS)]
            remote(sent, sent, sib_send.at[l * UNITS + u], ln_sib.at[1], dev_sib).wait_send()


def solution(mesh):
    batch_spec = P(("dp", "wg"))
    col_spec = P(None, None, "wg")
    out_spec = P(None, None, None, "wg")
    cache_spec = P(None, ("dp", "wg"))
    cols = math.isqrt(mesh.shape["dp"])
    chips = mesh.shape["wg"] // 2

    def local_program(x, positions, prompt_len, ln_attn, ln_mlp, w_qkv, w_out, w_up, w_down):
        prompts, seq, width = x.shape
        layers = w_qkv.shape[0]
        heads, head_dim = w_out.shape[1], w_out.shape[2]
        tokens = prompts * seq
        inv_freq = ROPE_BASE ** (-jnp.arange(head_dim // 2, dtype=F32) * 2.0 / head_dim)
        angles = inv_freq[:, None] * positions.astype(F32)[None, :]
        ln_rows = jnp.concatenate([ln_attn, ln_mlp], axis=1).astype(F32)
        ln_rows = jnp.pad(ln_rows, ((0, 0), (0, 8 - ln_rows.shape[1]), (0, 128 - ln_rows.shape[2])))
        qkv_t = jnp.swapaxes(w_qkv, 1, 2).reshape(layers, QUARTERS, -1, width)
        down_t = jnp.swapaxes(w_down, 1, 2).reshape(layers, QUARTERS, -1, w_down.shape[1])
        out_nat = w_out.reshape(layers, heads * head_dim, -1)
        up_rows = w_up.shape[2] // QUARTERS
        out_rows = out_nat.shape[2] // QUARTERS
        slots = chips * 2 * QUARTERS
        any_spec = pl.BlockSpec(memory_space=pl.ANY)
        vmem_spec = pl.BlockSpec(memory_space=pltpu.VMEM)
        cache = jax.ShapeDtypeStruct((layers, prompts, heads, head_dim, seq), BF16)
        dma = pltpu.SemaphoreType.DMA
        shares = chips * 2
        y, k_cache, v_cache = pl.pallas_call(
            functools.partial(kernel, cols, chips, layers),
            out_shape=(jax.ShapeDtypeStruct(x.shape, BF16), cache, cache),
            in_specs=[
                any_spec,
                vmem_spec,
                vmem_spec,
                pl.BlockSpec(memory_space=pltpu.SMEM),
                vmem_spec,
                any_spec,
                any_spec,
                any_spec,
                any_spec,
            ],
            out_specs=(vmem_spec, vmem_spec, vmem_spec),
            scratch_shapes=[
                pltpu.VMEM((layers, slots) + qkv_t.shape[2:], BF16),
                pltpu.VMEM((layers, slots, up_rows + out_rows, width), BF16),
                pltpu.VMEM((layers, slots) + down_t.shape[2:], BF16),
                pltpu.VMEM(w_up.shape, BF16),
                pltpu.VMEM(out_nat.shape, BF16),
                pltpu.VMEM(x.shape, BF16),
                pltpu.VMEM((shares, width // shares, tokens), BF16),
                pltpu.VMEM((width, tokens), BF16),
                pltpu.VMEM((width, tokens), BF16),
                pltpu.VMEM((heads, head_dim, tokens), BF16),
                pltpu.VMEM((shares, w_up.shape[2], tokens), BF16),
                pltpu.VMEM((shares, width // shares, tokens), F32),
                pltpu.VMEM((2, chips) + ln_rows.shape, F32),
                dma((layers * UNITS, 4, chips // 2)),
                dma((layers * UNITS, 2, chips - 1)),
                dma((layers * UNITS, chips)),
                dma((layers * UNITS, 2)),
                dma((layers * UNITS, 2)),
                dma((layers * UNITS,)),
                dma((2, chips // 2)),
                dma((2,)),
                dma((2,)),
                dma((2 * layers + 3,)),
            ],
            compiler_params=pltpu.CompilerParams(
                collective_id=0, has_side_effects=True, vmem_limit_bytes=67043328
            ),
        )(x, jnp.cos(angles), jnp.sin(angles), prompt_len, ln_rows, qkv_t, w_up, out_nat, down_t)
        order = (0, 1, 4, 2, 3)
        return y, k_cache.transpose(order), v_cache.transpose(order)

    return jax.shard_map(
        local_program,
        mesh=mesh,
        in_specs=(batch_spec, P("dp"), batch_spec, col_spec, col_spec, col_spec, out_spec, col_spec, col_spec),
        out_specs=(batch_spec, cache_spec, cache_spec),
        check_vma=False,
    )
```

time: 436 us -> 166 us (0.38)
  waiting for transfers between devices: 209 us -> 0 us
  Pallas kernels: 0 us -> 158 us
  blocking collectives: 78.9 us -> 0 us
  matrix products: 69.2 us -> 0 us
  other arithmetic: 34 us -> 1.37 us
  local copies, waits for them, and re-layouts: 25.6 us -> 5.86 us
  between operations: 14.7 us -> 0.66 us
    all_gather x8 -> x0, waiting for transfers between devices: 207 us -> none  [the longest x2 91.2 us: local_program(): up_full = lax.all_gather(w_up[layer_idx], 'wg', axis=1, tiled=True)]
    pallas_call x0 -> x1, Pallas kernels: none -> 158 us  [local_program(): pl.pallas_call(functools.partial(kernel, cols, chips, layers), out_shape=...]
    all_gather x4 -> x0, blocking collectives: 78.9 us -> none  [the longest x2 44.2 us: local_program(): ln_a = lax.all_gather(ln_attn[layer_idx], 'wg', axis=1, tiled=True)]
    dot_general x10 -> x0, matrix products: 69.2 us -> none  [the longest x2 28.7 us: decoder_layer(): jnp.einsum('bsf,fd->bsd', hidden, w_down, preferred_element_type=jnp.floa...]
    convert_element_type x5 -> x1, other arithmetic: 29.6 us -> 0.01 us  [local_program(): angles = inv_freq[:, None] * positions.astype(F32)[None, :]]
    all_gather x2 -> x0, local copies, waits for them, and re-layouts: 11.4 us -> none  [local_program(): out_full = lax.all_gather(w_out[layer_idx], 'wg', axis=2, tiled=True)]
    slice x6 -> x0, local copies, waits for them, and re-layouts: 5.35 us -> none  [the longest x1 2.04 us: local_program(): qkv_full = lax.all_gather(w_qkv[layer_idx], 'wg', axis=1, tiled=True)]
  transfers between devices with their start and end apart: 8 -> 0, of which waited for: 6 -> 0; matrix products, arithmetic and copies ran while one was open for 25% -> 0% of each run, Pallas kernels for 0% -> 0%
where the time goes in v1:
time: 166 us
  Pallas kernels  158 us (95%)
  local copies, waits for them, and re-layouts  5.86 us (4%)
    pallas_call x1, Pallas kernels, local_program(): pl.pallas_call(functools.partial(kernel, cols, chips, layers), out_shape=...  158 us
    unnamed x13, local copies, waits for them, and re-layouts  5.86 us

profile of v1, /device:TPU:21, one launch (start us, length us, event | category | flops | bytes accessed | tf_op | source)
XLA Modules:
  0.0 165.7 jit_solution(7999001734533020781)
XLA Ops:
  0.6 0.0 copy-start.4
  0.6 0.6 copy-done.4
  1.3 0.0 copy-start.3
  1.3 0.0 copy-start.2
  1.3 0.7 copy-done.3
  2.0 0.0 copy-done.2
  2.0 0.6 fusion.6.ln_ref
  2.6 0.8 multiply_sine_fusion
  3.3 157.8 %shard_map.112 = (bf16[2,128,1024]{2,1,0:T(8,128)(2,1)}, bf16[2,2,16,64,128]{4,3,2,1,0:T(8,128)(2,1)}, bf16[2,2,16,64,128]{4,3,2,1,0:T(8,128)(2,1)}) custom-call(bf16[2,128,1024]{2,1,0:T(8,128)(2,1)} %x_hbm.1, f32[32,128]{1,0:T(8,128)} %get-tuple-element.10.cos_ref, f32[32,128]{1,0:T(8,128)} %get-tuple-element.9.sin_ref, s32[2]{0:T(128)} %len_ref.1, ...), custom_call_target="tpu_custom_call" | custom-call | tf_op jit(solution)/shard_map/pallas_call | solution.py:390
  161.2 0.0 copy-start.1
  161.2 2.0 %copy.15 = bf16[2,128,1024]{2,1,0:T(8,128)(2,1)} copy(bf16[2,128,1024]{2,1,0:T(8,128)(2,1)} %get-tuple-element.14) | data formatting | bytes 1048576
  163.2 0.0 copy-done.1
  163.2 0.0 copy-start
  163.2 1.0 copy.16
  164.1 0.6 copy-done
  164.8 1.0 copy.17
  (2 shorter events, 0.0 us)
Async XLA Ops:
  0.6 0.7 copy-start.4
  1.3 0.7 copy-start.3
  1.3 0.7 copy-start.2
  161.2 2.0 %copy-start.1 = (bf16[2,2,16,64,128]{4,3,2,1,0:T(8,128)(2,1)S(1)}, bf16[2,2,16,64,128]{4,3,2,1,0:T(8,128)(2,1)}, u32[]{:S(2)}) copy-start(bf16[2,2,16,64,128]{4,3,2,1,0:T(8,128)(2,1)} %get-tuple-element.7) | copy-start | bytes 3145732
  163.2 1.6 copy-start

commit v2 on v1

--- a/solution.py
+++ b/solution.py
@@ -21,18 +21,18 @@
     cols,
     chips,
     layers,
+    pos_ref,
+    len_ref,
     x_hbm,
-    cos_ref,
-    sin_ref,
-    len_ref,
-    ln_ref,
+    lna_hbm,
+    lnm_hbm,
     qkv_hbm,
     up_hbm,
     out_hbm,
     down_hbm,
-    y_ref,
-    k_ref,
-    v_ref,
+    y_hbm,
+    k_hbm,
+    v_hbm,
     buf_q,
     buf_u,
     buf_d,
@@ -46,6 +46,12 @@
     hid_t,
     acc,
     ln_all,
+    ln_own,
+    ln_nat,
+    cos_ref,
+    sin_ref,
+    k_ref,
+    v_ref,
     z_recv,
     xy_recv,
     sib_recv,
@@ -56,6 +62,7 @@
     ln_send,
     ln_sib,
     load_sem,
+    cache_sem,
 ):
     half = chips // 2
     d_me = lax.axis_index("dp")
@@ -142,7 +149,7 @@
                 remote(ref, ref, ln_send.at[direction], ln_recv.at[direction, h - 1], dev_z[direction]).wait_recv()
             if h < limit:
                 dst = ln_all.at[c, chip_at(direction, h)]
-                src = ln_ref if h == 0 else dst
+                src = ln_own if h == 0 else dst
                 remote(src, dst, ln_send.at[direction], ln_recv.at[direction, h], dev_z[direction]).start()
 
     def ln_share(core):
@@ -238,30 +245,37 @@
     load_up = pltpu.make_async_copy(up_hbm, up_nat, load_sem.at[2 * layers])
     load_out = pltpu.make_async_copy(out_hbm, out_nat, load_sem.at[2 * layers + 1])
     load_x = pltpu.make_async_copy(x_hbm, x_nat, load_sem.at[2 * layers + 2])
-    loads[0].start()
-    load_x.start()
-    load_up.start()
-    load_out.start()
-    for load in loads[1:]:
+    load_ln = [pltpu.make_async_copy(src, ln_nat.at[i], load_sem.at[2 * layers + 3 + i]) for i, src in enumerate((lna_hbm, lnm_hbm))]
+    for load in [loads[0]] + load_ln + [load_x, load_up, load_out] + loads[1:]:
         load.start()
 
     barrier = pltpu.get_barrier_semaphore()
     neighbours = dev_z + dev_xy + (dev_sib,)
     for dev in neighbours:
         pl.semaphore_signal(barrier, inc=1, device_id=dev, device_id_type=MESH)
-    ln_all[c, z] = ln_ref[...]
+    ln_own[...] = jnp.zeros_like(ln_own)
+    for i in (0, 1):
+        load_ln[i].wait()
+        for l in range(layers):
+            ln_own[l, 2 * i : 2 * i + 2, : ln_nat.shape[3]] = ln_nat[i, l].astype(F32)
+    ln_all[c, z] = ln_own[...]
     loads[0].wait()
     pl.semaphore_wait(barrier, len(neighbours))
 
-    ln_hop(0)
     send_own(0, 0, 0)
     send_own(0, 0, 1)
+    ln_hop(0)
     send_own_sib(0, 0)
     load_x.wait()
     seq = x_hbm.shape[1]
     for b in range(x_hbm.shape[0]):
         x_t[:, :, b * seq : (b + 1) * seq] = x_nat[b].T.reshape(x_t.shape[0], x_t.shape[1], seq)
-    ln_hop(1)
+    half_dim = cos_ref.shape[0]
+    row = lax.broadcasted_iota(jnp.int32, cos_ref.shape, 0).astype(F32)
+    position = (pos_ref[0] + lax.broadcasted_iota(jnp.int32, cos_ref.shape, 1)).astype(F32)
+    angles = position * ROPE_BASE ** (-row * 2.0 / (2 * half_dim))
+    cos_ref[...] = jnp.cos(angles)
+    sin_ref[...] = jnp.sin(angles)
     load_up.wait()
     load_out.wait()
     up_rows = up_hbm.shape[2] // QUARTERS
@@ -273,74 +287,78 @@
         buf_u[l, own, up_rows:, :] = out_t.reshape(QUARTERS, -1, out_t.shape[-1])
 
     place_up(0)
-
-
-    order = [(u, h) for u in range(UNITS) for h in range(1, half + 1)]
-
-    def back(n, k):
-        return (order[n - k], 0) if n >= k else (order[n - k], -1)
-
-    @pl.loop(0, layers)
+    ln_hop(1)
+
+
+    period = 2 * UNITS
+    lands, shares, works = ([[] for _ in range(period)] for _ in range(3))
+    for h in range(1, half + 1):
+        for u in range(UNITS):
+            landing = 2 * u + h
+            work = 2 * u + half + (h > half // 2)
+            for table, n in ((lands, landing), (shares, landing + 1), (works, work)):
+                table[n % period].append((u, h, n // period))
+
+    def run(action, table, l):
+        for late in (0, 1):
+            items = [(u, h) for u, h, lateness in table if lateness == late]
+            if items:
+
+                @pl.when(l < layers if late == 0 else l > 0)
+                def _():
+                    for u, h in items:
+                        action(l - late, u, h)
+
+    def land(l, u, h):
+        forward(l, u, h, 0)
+        forward(l, u, h, 1)
+
+    def work(l, u, h):
+        compute(l, u, h)
+        if u == 0 and h == half:
+            for copy in cache_copies(l):
+                copy.start()
+
+    def cache_copies(l):
+        return [
+            pltpu.make_async_copy(src.at[l], dst.at[l], cache_sem.at[l, i])
+            for i, (src, dst) in enumerate(((k_ref, k_hbm), (v_ref, v_hbm)))
+        ]
+
+    @pl.loop(0, layers + 1)
     def _(l):
-        first = l == 0
-
-        def lagged(action, n, k):
-            (u, h), offset = back(n, k)
-            if offset == 0:
-                action(l, u, h)
-            else:
-
-                @pl.when(l > 0)
+        for n in range(period):
+            if n % 2 == 0:
+                u = n // 2
+
+                @pl.when((l < layers) & (l + u > 0))
                 def _():
-                    action(l - 1, u, h)
-
-        for n, (u, h) in enumerate(order):
-            if u == 0 and h <= 2:
-
-                @pl.when(first)
+                    for s in (0, 1):
+                        send_own(l, u, s)
+                    send_own_sib(l, u)
+
+            run(land, lands[n], l)
+            if n in (1, 2, 3):
+
+                @pl.when(l == 0)
                 def _():
-                    ln_hop(2 * h)
-
-            forward(l, u, h, 0)
-            if u == 0 and h == 1:
-
-                @pl.when(first)
-                def _():
-                    ln_hop(3)
-
-            forward(l, u, h, 1)
-            if u == 0 and h == 2:
-
-                @pl.when(first)
-                def _():
-                    ln_share(c).start()
-                    for load in loads[1:]:
-                        load.wait()
-                    place_up(1)
-
-            if h == half - 1:
-                if u + 1 < UNITS:
-                    for s in (0, 1):
-                        send_own(l, u + 1, s)
-                    send_own_sib(l, u + 1)
-                else:
-
-                    @pl.when(l + 1 < layers)
-                    def _():
-                        for s in (0, 1):
-                            send_own(l + 1, 0, s)
-                        send_own_sib(l + 1, 0)
-
-            lagged(share_with_sibling, n, 1)
-            lagged(compute, n, 2)
-
-    last = layers - 1
-    share_with_sibling(last, UNITS - 1, half)
-    compute(last, UNITS - 1, half - 1)
-    compute(last, UNITS - 1, half)
+                    ln_hop(n + 1)
+                    if n == 2:
+                        for load in loads[1:]:
+                            load.wait()
+                        for later in range(1, layers):
+                            place_up(later)
+                    if n == 3:
+                        ln_share(c).start()
+
+            run(share_with_sibling, shares[n], l)
+            run(work, works[n], l)
+
     y_t = x_t[...].reshape(-1, x_t.shape[-1])
-    for b in range(y_ref.shape[0]):
-        y_ref[b] = y_t[:, b * seq : (b + 1) * seq].T
+    for b in range(x_hbm.shape[0]):
+        x_nat[b] = y_t[:, b * seq : (b + 1) * seq].T
+    store_y = pltpu.make_async_copy(x_nat, y_hbm, load_sem.at[2 * layers + 2])
+    store_y.start()
 
     ref = ln_all.at[c]
     for direction in (0, 1):
@@ -357,6 +375,10 @@
                 remote(sent, sent, xy_send.at[l * UNITS + u, i], ln_sib.at[1], dev_xy[i]).wait_send()
             sent = bufs[u].at[l, pl.ds(0, chips * QUARTERS)]
             remote(sent, sent, sib_send.at[l * UNITS + u], ln_sib.at[1], dev_sib).wait_send()
+        for copy in cache_copies(l):
+            copy.wait()
+
+    store_y.wait()
 
 
 def solution(mesh):
@@ -372,10 +394,6 @@
         layers = w_qkv.shape[0]
         heads, head_dim = w_out.shape[1], w_out.shape[2]
         tokens = prompts * seq
-        inv_freq = ROPE_BASE ** (-jnp.arange(head_dim // 2, dtype=F32) * 2.0 / head_dim)
-        angles = inv_freq[:, None] * positions.astype(F32)[None, :]
-        ln_rows = jnp.concatenate([ln_attn, ln_mlp], axis=1).astype(F32)
-        ln_rows = jnp.pad(ln_rows, ((0, 0), (0, 8 - ln_rows.shape[1]), (0, 128 - ln_rows.shape[2])))
         qkv_t = jnp.swapaxes(w_qkv, 1, 2).reshape(layers, QUARTERS, -1, width)
         down_t = jnp.swapaxes(w_down, 1, 2).reshape(layers, QUARTERS, -1, w_down.shape[1])
         out_nat = w_out.reshape(layers, heads * head_dim, -1)
@@ -383,25 +401,14 @@
         out_rows = out_nat.shape[2] // QUARTERS
         slots = chips * 2 * QUARTERS
         any_spec = pl.BlockSpec(memory_space=pl.ANY)
-        vmem_spec = pl.BlockSpec(memory_space=pltpu.VMEM)
         cache = jax.ShapeDtypeStruct((layers, prompts, heads, head_dim, seq), BF16)
         dma = pltpu.SemaphoreType.DMA
         shares = chips * 2
         y, k_cache, v_cache = pl.pallas_call(
             functools.partial(kernel, cols, chips, layers),
             out_shape=(jax.ShapeDtypeStruct(x.shape, BF16), cache, cache),
-            in_specs=[
-                any_spec,
-                vmem_spec,
-                vmem_spec,
-                pl.BlockSpec(memory_space=pltpu.SMEM),
-                vmem_spec,
-                any_spec,
-                any_spec,
-                any_spec,
-                any_spec,
-            ],
-            out_specs=(vmem_spec, vmem_spec, vmem_spec),
+            in_specs=[pl.BlockSpec(memory_space=pltpu.SMEM)] * 2 + [any_spec] * 7,
+            out_specs=(any_spec,) * 3,
             scratch_shapes=[
                 pltpu.VMEM((layers, slots) + qkv_t.shape[2:], BF16),
                 pltpu.VMEM((layers, slots, up_rows + out_rows, width), BF16),
@@ -415,7 +422,13 @@
                 pltpu.VMEM((heads, head_dim, tokens), BF16),
                 pltpu.VMEM((shares, w_up.shape[2], tokens), BF16),
                 pltpu.VMEM((shares, width // shares, tokens), F32),
-                pltpu.VMEM((2, chips) + ln_rows.shape, F32),
+                pltpu.VMEM((2, chips, layers, 8, 128), F32),
+                pltpu.VMEM((layers, 8, 128), F32),
+                pltpu.VMEM((2,) + ln_attn.shape, BF16),
+                pltpu.VMEM((head_dim // 2, seq), F32),
+                pltpu.VMEM((head_dim // 2, seq), F32),
+                pltpu.VMEM(cache.shape, BF16),
+                pltpu.VMEM(cache.shape, BF16),
                 dma((layers * UNITS, 4, chips // 2)),
                 dma((layers * UNITS, 2, chips - 1)),
                 dma((layers * UNITS, chips)),
@@ -425,12 +438,13 @@
                 dma((2, chips // 2)),
                 dma((2,)),
                 dma((2,)),
-                dma((2 * layers + 3,)),
+                dma((2 * layers + 5,)),
+                dma((layers, 2)),
             ],
             compiler_params=pltpu.CompilerParams(
                 collective_id=0, has_side_effects=True, vmem_limit_bytes=67043328
             ),
-        )(x, jnp.cos(angles), jnp.sin(angles), prompt_len, ln_rows, qkv_t, w_up, out_nat, down_t)
+        )(positions, prompt_len, x, ln_attn, ln_mlp, qkv_t, w_up, out_nat, down_t)
         order = (0, 1, 4, 2, 3)
         return y, k_cache.transpose(order), v_cache.transpose(order)
 

time: 166 us -> 156 us (0.940)
  Pallas kernels: 158 us -> 151 us
    pallas_call x1, Pallas kernels: 158 us -> 151 us  [local_program(): pl.pallas_call(functools.partial(kernel, cols, chips, layers), out_shape=...]
    unnamed x13 -> x7, local copies, waits for them, and re-layouts: 5.86 us -> 4.53 us
where the time goes in v2:
time: 156 us
  Pallas kernels  151 us (97%)
  local copies, waits for them, and re-layouts  4.53 us (3%)
    pallas_call x1, Pallas kernels, local_program(): pl.pallas_call(functools.partial(kernel, cols, chips, layers), out_shape=...  151 us
    unnamed x7, local copies, waits for them, and re-layouts  4.53 us

profile of v2, /device:TPU:21, one launch (start us, length us, event | category | flops | bytes accessed | tf_op | source)
XLA Modules:
  0.0 155.7 jit_solution(2129869019910927048)
XLA Ops:
  0.6 150.6 %shard_map.112 = (bf16[2,128,1024]{2,1,0:T(8,128)(2,1)}, bf16[2,2,16,64,128]{4,3,2,1,0:T(8,128)(2,1)}, bf16[2,2,16,64,128]{4,3,2,1,0:T(8,128)(2,1)}) custom-call(s32[128]{0:T(128)} %pos_ref.1, s32[2]{0:T(128)} %len_ref.1, bf16[2,128,1024]{2,1,0:T(8,128)(2,1)} %x_hbm.1, bf16[2,2,64]{2,1,0:T(2,128)(2,1)} %lna_hbm.1, bf16[2,2,64]{2,1,0:T(2,128)(2,1)} %lnm_hbm.1, ...), custom_call_target="tpu_custom_call" | custom-call | tf_op jit(solution)/shard_map/pallas_call | solution.py:407
  151.2 0.0 copy-start.1
  151.2 2.0 %copy.15 = bf16[2,128,1024]{2,1,0:T(8,128)(2,1)} copy(bf16[2,128,1024]{2,1,0:T(8,128)(2,1)} %get-tuple-element.12) | data formatting | bytes 1048576
  153.2 0.0 copy-done.1
  153.2 0.0 copy-start
  153.2 1.0 copy.16
  154.1 0.6 copy-done
  154.8 1.0 copy.17
Async XLA Ops:
  151.2 2.0 %copy-start.1 = (bf16[2,2,16,64,128]{4,3,2,1,0:T(8,128)(2,1)S(1)}, bf16[2,2,16,64,128]{4,3,2,1,0:T(8,128)(2,1)}, u32[]{:S(2)}) copy-start(bf16[2,2,16,64,128]{4,3,2,1,0:T(8,128)(2,1)} %get-tuple-element.7) | copy-start | bytes 3145732
  153.2 1.6 %copy-start = (bf16[2,2,16,64,128]{4,3,2,1,0:T(8,128)(2,1)S(1)}, bf16[2,2,16,64,128]{4,3,2,1,0:T(8,128)(2,1)}, u32[]{:S(2)}) copy-start(bf16[2,2,16,64,128]{4,3,2,1,0:T(8,128)(2,1)} %get-tuple-element.8) | copy-start | bytes 3145732

commit v3 on v2

v3 whole, which is shorter than its diff:
```python
import functools
import math

import jax
import jax.numpy as jnp
from jax import lax
from jax.experimental import pallas as pl
from jax.experimental.pallas import tpu as pltpu
from jax.sharding import PartitionSpec as P

EPSILON = 1e-5
ROPE_BASE = 10000.0
MESH = pl.DeviceIdType.MESH
F32 = jnp.float32
BF16 = jnp.bfloat16
QUARTERS = 4
HALF_UP, HALF_DOWN, QKV_0, QKV_1, UP, DOWN = range(6)
UNITS = 6
X_LINK, Y_LINK = 0, 1


def kernel(
    cols,
    chips,
    pos_ref,
    len_ref,
    x_hbm,
    lna_hbm,
    lnm_hbm,
    qkv_hbm,
    up_hbm,
    out_hbm,
    down_hbm,
    y_hbm,
    k_hbm,
    v_hbm,
    buf_hu,
    buf_hd,
    buf_q0,
    buf_q1,
    buf_u,
    buf_d,
    up_half,
    up_nat,
    out_nat,
    x_nat,
    x_other,
    x_t,
    x_other_t,
    a_t,
    m_t,
    ctx_t,
    hid_half,
    hid_t,
    acc,
    part_out,
    part_in,
    ln_all,
    ln_own,
    ln_nat,
    cos_ref,
    sin_ref,
    k_ref,
    v_ref,
    z_recv,
    xy_recv,
    sib_recv,
    part_recv,
    z_send,
    xy_send,
    sib_send,
    part_send,
    ln_recv,
    ln_send,
    ln_sib,
    x_sem,
    load_sem,
    cache_sem,
):
    half = chips // 2
    shares = 2 * chips
    tokens = x_t.shape[-1]
    seq = k_ref.shape[4]
    prompts = k_ref.shape[1]
    layers = k_ref.shape[0]
    d_me = lax.axis_index("dp")
    w_me = lax.axis_index("wg")
    z, c = w_me // 2, w_me % 2
    px, py = (d_me // cols) % 2, (d_me % cols) % 2
    dev_z = ({"wg": lax.rem(z + 1, chips) * 2 + c}, {"wg": lax.rem(z + chips - 1, chips) * 2 + c})
    dev_xy = ({"dp": d_me + cols * (1 - 2 * px)}, {"dp": d_me + 1 - 2 * py})
    dev_sib = {"wg": z * 2 + 1 - c}
    bufs = (buf_hu, buf_hd, buf_q0, buf_q1, buf_u, buf_d)
    hops = ((half, half - 1), (half - 1, half))

    by_quarter = (((px, 1), X_LINK, (1 - px, 1)), ((2 + py, 1), Y_LINK, (3 - py, 1)))
    plans = (
        (((0, 1), None, None), ((1 + px, 1), X_LINK, (2 - px, 1))),
        (((0, 2), None, None), ((2 + px, 1), X_LINK, (3 - px, 1))),
    ) + (by_quarter,) * 4

    def chip_at(direction, h):
        return lax.rem(z + chips - h, chips) if direction == 0 else lax.rem(z + h, chips)

    def pieces(u, chip, which):
        return bufs[u].at[chip * 2 + c, pl.ds(which[0], which[1])]

    def remote(src, dst, send, recv, dev):
        return pltpu.make_async_remote_copy(
            src_ref=src, dst_ref=dst, send_sem=send, recv_sem=recv, device_id=dev, device_id_type=MESH
        )

    def z_link(u, direction, s, h, chip):
        ref = pieces(u, chip, plans[u][s][0])
        return remote(ref, ref, z_send.at[u, direction], z_recv.at[u, direction * 2 + s, h - 1], dev_z[direction])

    def z_copy(u, direction, s, h):
        return z_link(u, direction, s, h, chip_at(direction, h - 1))

    def z_arrival(u, direction, s, h):
        return z_link(u, direction, s, h, chip_at(direction, h))

    def source_index(direction, h):
        return (h - 1) * 2 + direction if h < half else chips - 2

    def xy_copy(u, direction, s, h, which):
        ref = pieces(u, chip_at(direction, h), which)
        link = plans[u][s][1]
        return remote(ref, ref, xy_send.at[u, s], xy_recv.at[u, s, source_index(direction, h)], dev_xy[link])

    def sib_copy(u, chip, core, index):
        ref = bufs[u].at[chip * 2 + core]
        return remote(ref, ref, sib_send.at[u], sib_recv.at[u, index], dev_sib)

    def send_own(u):
        for s in (0, 1):
            for direction in (0, 1):
                z_copy(u, direction, s, 1).start()
        sib_copy(u, z, c, chips - 1).start()

    def land(u, h):
        for s in (0, 1):
            for direction in (0, 1):
                if h > hops[direction][s]:
                    continue
                z_arrival(u, direction, s, h).wait_recv()
                if h < hops[direction][s]:
                    z_copy(u, direction, s, h + 1).start()
                if plans[u][s][1] is not None:
                    xy_copy(u, direction, s, h, plans[u][s][0]).start()

    def sources(h):
        return (0, 1) if h < half else (0,)

    def share_with_sibling(u, h):
        for direction in sources(h):
            for s in (0, 1):
                if plans[u][s][1] is not None:
                    xy_copy(u, direction, s, h, plans[u][s][2]).wait_recv()
            sib_copy(u, chip_at(direction, h), c, source_index(direction, h)).start()

    def wait_sibling(u, h):
        for direction in sources(h):
            sib_copy(u, chip_at(direction, h), 1 - c, source_index(direction, h)).wait_recv()
        if h == half:
            sib_copy(u, z, 1 - c, chips - 1).wait_recv()

    def chip_pair(h, i):
        return lax.rem(z + (chips - h + i * 2 * h if h < half else half + i * half), chips)

    def ln_hop(h):
        for direction in (0, 1):
            limit = half - direction
            if h > limit:
                continue
            ref = ln_all.at[c, chip_at(direction, h)]
            if h > 0:
                remote(ref, ref, ln_send.at[direction], ln_recv.at[direction, h - 1], dev_z[direction]).wait_recv()
            if h < limit:
                src = ln_own if h == 0 else ref
                remote(src, ref, ln_send.at[direction], ln_recv.at[direction, h], dev_z[direction]).start()

    def ln_share(core):
        return remote(ln_all.at[core], ln_all.at[core], ln_sib.at[0], ln_sib.at[1], dev_sib)

    def send_x():
        return remote(x_nat, x_other, x_sem.at[0], x_sem.at[1], dev_xy[Y_LINK])

    def part_copy(chip):
        return remote(part_out.at[chip], part_in.at[chip], part_send.at[0], part_recv.at[chip], dev_xy[Y_LINK])


    def transpose_tokens(dst, src):
        for b in range(prompts):
            dst[:, :, b * seq : (b + 1) * seq] = src[b].T.reshape(dst.shape[0], dst.shape[1], seq)

    def normalize(l, src, first, a_dst):
        rows = src[...].reshape(-1, tokens).astype(F32)
        centered = rows - jnp.mean(rows, axis=0, keepdims=True)
        var = jnp.mean(centered * centered, axis=0, keepdims=True)
        normed = centered * lax.rsqrt(var + EPSILON)
        params = ln_all[:, :, l].reshape(-1, 128).T
        step = src.shape[1]
        for w in range(shares):
            block = normed[w * step : (w + 1) * step]
            base = ((w % 2) * chips + w // 2) * 8
            column = [params[:step, base + r : base + r + 1] for r in range(4)]
            if a_dst is not None:
                a_dst[w * step : (w + 1) * step, :] = (block * column[0] + column[1]).astype(BF16)
            m_t[w * step : (w + 1) * step, first : first + tokens] = (block * column[2] + column[3]).astype(BF16)

    def gelu(pre):
        return (0.5 * pre * (1.0 + lax.erf(pre * 0.5**0.5))).astype(BF16)

    def rotate(vec, cos, sin):
        first, second = vec[: cos.shape[0]].astype(F32), vec[cos.shape[0] :].astype(F32)
        return jnp.concatenate([first * cos - second * sin, second * cos + first * sin], axis=0).astype(BF16)

    def compute_qkv(l, buf, chip):
        head_dim = k_ref.shape[3]
        cos, sin = cos_ref[...], sin_ref[...]
        k_index = lax.broadcasted_iota(jnp.int32, (seq, seq), 0)
        q_index = lax.broadcasted_iota(jnp.int32, (seq, seq), 1)
        for core in (0, 1):
            head = chip * 2 + core
            share = buf[head].reshape(-1, buf.shape[-1])
            qkv = jnp.dot(share, a_t[...], preferred_element_type=F32).astype(BF16)
            for b in range(prompts):
                cols_b = slice(b * seq, (b + 1) * seq)
                q_t = rotate(qkv[:head_dim, cols_b], cos, sin)
                k_t = rotate(qkv[head_dim : 2 * head_dim, cols_b], cos, sin)
                v_t = qkv[2 * head_dim :, cols_b]
                k_ref[l, b, head] = k_t
                v_ref[l, b, head] = v_t
                scores = jnp.dot(k_t.T, q_t, preferred_element_type=F32) * head_dim**-0.5
                allowed = (k_index <= q_index) & (k_index < len_ref[b])
                scores = jnp.where(allowed, scores, -1e30)
                top = jnp.max(scores, axis=0, keepdims=True)
                expo = jnp.exp(scores - top)
                prob = (expo * (1.0 / jnp.sum(expo, axis=0, keepdims=True))).astype(BF16)
                ctx_t[head, :, cols_b] = jnp.dot(v_t, prob, preferred_element_type=F32).astype(BF16)

    def compute_half_up(chip):
        both = pl.ds(chip * 2, 2)
        share = buf_hu[both, 1:].reshape(-1, buf_hu.shape[-1])
        for i in (0, 1):
            cols_i = slice(i * tokens, (i + 1) * tokens)
            pre = jnp.dot(share, m_t[:, cols_i], preferred_element_type=F32)
            hid_half[both, :, cols_i] = gelu(pre).reshape(2, -1, tokens)

    def compute_half_down(chip):
        both = pl.ds(chip * 2, 2)
        share = buf_hd[both].reshape(-1, buf_hd.shape[-1])
        hidden = hid_half[...].reshape(-1, 2 * tokens)
        acc[both] = jnp.dot(share, hidden[:, :tokens], preferred_element_type=F32).reshape((2,) + acc.shape[1:])
        part = jnp.dot(share, hidden[:, tokens:], preferred_element_type=F32)
        part_out[chip] = part.reshape(part_out.shape[1:])

    def finish_layer_0():
        @pl.loop(0, chips)
        def _(chip):
            part_copy(chip).wait_recv()
            both = pl.ds(chip * 2, 2)
            share = buf_hu[both, 0].reshape(-1, buf_hu.shape[-1])
            attn_out = jnp.dot(share, ctx_t[...].reshape(-1, tokens), preferred_element_type=F32)
            mlp_out = acc[both] + part_in[chip]
            x_t[both] = (x_t[both].astype(F32) + attn_out.reshape(mlp_out.shape) + mlp_out).astype(BF16)

    def compute_up(chip):
        up_rows = up_hbm.shape[2] // QUARTERS
        for core in (0, 1):
            share = buf_u[chip * 2 + core, :, :up_rows, :].reshape(-1, buf_u.shape[-1])
            hid_t[chip * 2 + core] = gelu(jnp.dot(share, m_t[:, :tokens], preferred_element_type=F32))
        both = pl.ds(chip * 2, 2)
        share = buf_u[both, :, up_rows:, :].reshape(-1, buf_u.shape[-1])
        attn_out = jnp.dot(share, ctx_t[...].reshape(-1, tokens), preferred_element_type=F32)
        acc[both] = attn_out.reshape((2,) + acc.shape[1:])

    def compute_down(chip):
        both = pl.ds(chip * 2, 2)
        share = buf_d[both].reshape(-1, buf_d.shape[-1])
        hidden = hid_t[...].reshape(-1, tokens)
        mlp_out = jnp.dot(share, hidden, preferred_element_type=F32).reshape((2,) + acc.shape[1:])
        x_t[both] = (x_t[both].astype(F32) + acc[both] + mlp_out).astype(BF16)

    computes = (
        compute_half_up,
        compute_half_down,
        functools.partial(compute_qkv, 0, buf_q0),
        functools.partial(compute_qkv, 1, buf_q1),
        compute_up,
        compute_down,
    )

    def cache_copies(l):
        return [
            pltpu.make_async_copy(src.at[l], dst.at[l], cache_sem.at[l, i])
            for i, (src, dst) in enumerate(((k_ref, k_hbm), (v_ref, v_hbm)))
        ]

    def work(u, h):
        wait_sibling(u, h)
        if (u, h) == (HALF_UP, 1):
            ln_share(1 - c).wait_recv()
            normalize(0, x_t, 0, a_t)
            send_x().wait_recv()
            transpose_tokens(x_other_t, x_other)
            normalize(0, x_other_t, tokens, None)
        if (u, h) == (QKV_1, 1):
            finish_layer_0()
            normalize(1, x_t, 0, a_t)

        @pl.loop(0, 2)
        def _(i):
            computes[u](chip_pair(h, i))

        if h == half and u in (QKV_0, QKV_1):
            for copy in cache_copies(u - QKV_0):
                copy.start()

    def ship(h):
        @pl.loop(0, 2)
        def _(i):
            part_copy(chip_pair(h, i)).start()


    own_half = up_half.shape[1]
    loads = [
        pltpu.make_async_copy(up_hbm.at[0, :, pl.ds(py * own_half, own_half)], up_half, load_sem.at[0]),
        pltpu.make_async_copy(out_hbm, out_nat, load_sem.at[1]),
        pltpu.make_async_copy(x_hbm, x_nat, load_sem.at[2]),
        pltpu.make_async_copy(lna_hbm, ln_nat.at[0], load_sem.at[3]),
        pltpu.make_async_copy(lnm_hbm, ln_nat.at[1], load_sem.at[4]),
        pltpu.make_async_copy(up_hbm.at[1], up_nat, load_sem.at[5]),
        pltpu.make_async_copy(qkv_hbm.at[0], buf_q0.at[w_me], load_sem.at[6]),
        pltpu.make_async_copy(qkv_hbm.at[1], buf_q1.at[w_me], load_sem.at[7]),
        pltpu.make_async_copy(down_hbm.at[1], buf_d.at[w_me], load_sem.at[8]),
    ]
    for load in loads[:5]:
        load.start()
    for w in range(shares):
        pltpu.make_async_copy(
            down_hbm.at[0, :, :, pl.ds(w * 2 * own_half + py * own_half, own_half)],
            buf_hd.at[w_me, :, :, pl.ds(w * own_half, own_half)],
            load_sem.at[9],
        ).start()
    for load in loads[5:]:
        load.start()

    barrier = pltpu.get_barrier_semaphore()
    neighbours = dev_z + dev_xy + (dev_sib,)
    for dev in neighbours:
        pl.semaphore_signal(barrier, inc=1, device_id=dev, device_id_type=MESH)
    loads[0].wait()
    loads[1].wait()
    buf_hu[w_me, 0] = out_nat[0].T
    buf_hu[w_me, 1:] = up_half[...].T.reshape(buf_hu.shape[1] - 1, buf_hu.shape[2], buf_hu.shape[3])
    ln_own[...] = jnp.zeros_like(ln_own)
    for i in (0, 1):
        loads[3 + i].wait()
        for l in range(layers):
            ln_own[l, 2 * i : 2 * i + 2, : ln_nat.shape[3]] = ln_nat[i, l].astype(F32)
    ln_all[c, z] = ln_own[...]
    loads[2].wait()
    pl.semaphore_wait(barrier, len(neighbours))

    send_x().start()
    send_own(0)
    ln_hop(0)
    transpose_tokens(x_t, x_nat)
    half_dim = cos_ref.shape[0]
    row = lax.broadcasted_iota(jnp.int32, cos_ref.shape, 0).astype(F32)
    position = (pos_ref[0] + lax.broadcasted_iota(jnp.int32, cos_ref.shape, 1)).astype(F32)
    angles = position * ROPE_BASE ** (-row * 2.0 / (2 * half_dim))
    cos_ref[...] = jnp.cos(angles)
    sin_ref[...] = jnp.sin(angles)
    ln_hop(1)
    for load in loads[5:]:
        load.wait()
    pltpu.make_async_copy(buf_hd.at[w_me], buf_hd.at[w_me], load_sem.at[9]).wait()
    up_rows = up_hbm.shape[2] // QUARTERS


    lands, gives, works = ([[] for _ in range(2 * UNITS + half)] for _ in range(3))
    for h in range(1, half + 1):
        for u in range(UNITS):
            lands[2 * u + h].append((u, h))
            gives[2 * u + h + 1].append((u, h))
            works[2 * u + half + (h > half // 2)].append((u, h))

    unshipped = []
    for n in range(2 * UNITS + half):
        if n % 2 == 0 and 0 < n < 2 * UNITS:
            send_own(n // 2)
        for u, h in lands[n]:
            land(u, h)
        if n in (1, 2, 3):
            ln_hop(n + 1)
        if n == 2:
            buf_u[w_me, :, :up_rows, :] = up_nat[...].T.reshape(QUARTERS, up_rows, -1)
            buf_u[w_me, :, up_rows:, :] = out_nat[1].T.reshape(QUARTERS, -1, buf_u.shape[-1])
        if n == 3:
            ln_share(c).start()
        for u, h in gives[n]:
            share_with_sibling(u, h)
        for h in unshipped:
            ship(h)
        unshipped = []
        for u, h in works[n]:
            work(u, h)
            for earlier in unshipped:
                ship(earlier)
            unshipped = [h] if u == HALF_DOWN else []

    send_x().wait_send()
    y_t = x_t[...].reshape(-1, tokens)
    for b in range(prompts):
        x_nat[b] = y_t[:, b * seq : (b + 1) * seq].T
    store_y = pltpu.make_async_copy(x_nat, y_hbm, load_sem.at[2])
    store_y.start()

    for direction in (0, 1):
        src = ln_all.at[c, pl.ds(0, half - direction)]
        remote(src, src, ln_send.at[direction], ln_sib.at[1], dev_z[direction]).wait_send()
    ln_share(c).wait_send()
    remote(part_out, part_in, part_send.at[0], ln_sib.at[1], dev_xy[Y_LINK]).wait_send()
    for u in range(UNITS):
        for direction in (0, 1):
            count = sum(hops[direction][s] * plans[u][s][0][1] for s in (0, 1))
            sent = bufs[u].at[pl.ds(0, count), 0]
            remote(sent, sent, z_send.at[u, direction], ln_sib.at[1], dev_z[direction]).wait_send()
        for s in (0, 1):
            if plans[u][s][1] is not None:
                sent = bufs[u].at[pl.ds(0, chips - 1), 0]
                remote(sent, sent, xy_send.at[u, s], ln_sib.at[1], dev_xy[plans[u][s][1]]).wait_send()
        sent = bufs[u].at[pl.ds(0, chips)]
        remote(sent, sent, sib_send.at[u], ln_sib.at[1], dev_sib).wait_send()
    for l in range(layers):
        for copy in cache_copies(l):
            copy.wait()
    store_y.wait()


def solution(mesh):
    batch_spec = P(("dp", "wg"))
    col_spec = P(None, None, "wg")
    out_spec = P(None, None, None, "wg")
    cache_spec = P(None, ("dp", "wg"))
    cols = math.isqrt(mesh.shape["dp"])
    chips = mesh.shape["wg"] // 2

    def local_program(x, positions, prompt_len, ln_attn, ln_mlp, w_qkv, w_out, w_up, w_down):
        prompts, seq, width = x.shape
        layers = w_qkv.shape[0]
        heads, head_dim = w_out.shape[1], w_out.shape[2]
        tokens = prompts * seq
        qkv_t = jnp.swapaxes(w_qkv, 1, 2).reshape(layers, QUARTERS, -1, width)
        down_t = jnp.swapaxes(w_down, 1, 2).reshape(layers, QUARTERS, -1, w_down.shape[1])
        out_nat = w_out.reshape(layers, heads * head_dim, -1)
        up_rows = w_up.shape[2] // QUARTERS
        out_rows = out_nat.shape[2] // QUARTERS
        half_up = w_up.shape[2] // 2
        any_spec = pl.BlockSpec(memory_space=pl.ANY)
        cache = jax.ShapeDtypeStruct((layers, prompts, heads, head_dim, seq), BF16)
        dma = pltpu.SemaphoreType.DMA
        shares = chips * 2
        y, k_cache, v_cache = pl.pallas_call(
            functools.partial(kernel, cols, chips),
            out_shape=(jax.ShapeDtypeStruct(x.shape, BF16), cache, cache),
            in_specs=[pl.BlockSpec(memory_space=pltpu.SMEM)] * 2 + [any_spec] * 7,
            out_specs=(any_spec,) * 3,
            scratch_shapes=[
                pltpu.VMEM((shares, 3, half_up // 2, width), BF16),
                pltpu.VMEM((shares, QUARTERS, down_t.shape[2], down_t.shape[3] // 2), BF16),
                pltpu.VMEM((shares,) + qkv_t.shape[1:], BF16),
                pltpu.VMEM((shares,) + qkv_t.shape[1:], BF16),
                pltpu.VMEM((shares, QUARTERS, up_rows + out_rows, width), BF16),
                pltpu.VMEM((shares,) + down_t.shape[1:], BF16),
                pltpu.VMEM((width, half_up), BF16),
                pltpu.VMEM(w_up.shape[1:], BF16),
                pltpu.VMEM(out_nat.shape, BF16),
                pltpu.VMEM(x.shape, BF16),
                pltpu.VMEM(x.shape, BF16),
                pltpu.VMEM((shares, width // shares, tokens), BF16),
                pltpu.VMEM((shares, width // shares, tokens), BF16),
                pltpu.VMEM((width, tokens), BF16),
                pltpu.VMEM((width, 2 * tokens), BF16),
                pltpu.VMEM((heads, head_dim, tokens), BF16),
                pltpu.VMEM((shares, half_up, 2 * tokens), BF16),
                pltpu.VMEM((shares, w_up.shape[2], tokens), BF16),
                pltpu.VMEM((shares, width // shares, tokens), F32),
                pltpu.VMEM((chips, 2, width // shares, tokens), F32),
                pltpu.VMEM((chips, 2, width // shares, tokens), F32),
                pltpu.VMEM((2, chips, layers, 8, 128), F32),
                pltpu.VMEM((layers, 8, 128), F32),
                pltpu.VMEM((2,) + ln_attn.shape, BF16),
                pltpu.VMEM((head_dim // 2, seq), F32),
                pltpu.VMEM((head_dim // 2, seq), F32),
                pltpu.VMEM(cache.shape, BF16),
                pltpu.VMEM(cache.shape, BF16),
                dma((UNITS, 4, chips // 2)),
                dma((UNITS, 2, chips - 1)),
                dma((UNITS, chips)),
                dma((chips,)),
                dma((UNITS, 2)),
                dma((UNITS, 2)),
                dma((UNITS,)),
                dma((1,)),
                dma((2, chips // 2)),
                dma((2,)),
                dma((2,)),
                dma((2,)),
                dma((10,)),
                dma((layers, 2)),
            ],
            compiler_params=pltpu.CompilerParams(
                collective_id=0, has_side_effects=True, vmem_limit_bytes=67043328
            ),
        )(positions, prompt_len, x, ln_attn, ln_mlp, qkv_t, w_up, out_nat, down_t)
        order = (0, 1, 4, 2, 3)
        return y, k_cache.transpose(order), v_cache.transpose(order)

    return jax.shard_map(
        local_program,
        mesh=mesh,
        in_specs=(batch_spec, P("dp"), batch_spec, col_spec, col_spec, col_spec, out_spec, col_spec, col_spec),
        out_specs=(batch_spec, cache_spec, cache_spec),
        check_vma=False,
    )
```

time: 156 us -> 164 us (1.051)
  Pallas kernels: 151 us -> 159 us
    pallas_call x1, Pallas kernels: 151 us -> 159 us  [local_program(): pl.pallas_call(functools.partial(kernel, cols, chips), out_shape=(jax.Sha...]
where the time goes in v3:
time: 164 us
  Pallas kernels  159 us (97%)
  local copies, waits for them, and re-layouts  4.53 us (3%)
    pallas_call x1, Pallas kernels, local_program(): pl.pallas_call(functools.partial(kernel, cols, chips), out_shape=(jax.Sha...  159 us
    unnamed x7, local copies, waits for them, and re-layouts  4.53 us

profile of v3, /device:TPU:21, one launch (start us, length us, event | category | flops | bytes accessed | tf_op | source)
XLA Modules:
  0.0 164.0 jit_solution(7836881767886865571)
XLA Ops:
  0.6 158.8 %shard_map.112 = (bf16[2,128,1024]{2,1,0:T(8,128)(2,1)}, bf16[2,2,16,64,128]{4,3,2,1,0:T(8,128)(2,1)}, bf16[2,2,16,64,128]{4,3,2,1,0:T(8,128)(2,1)}) custom-call(s32[128]{0:T(128)} %pos_ref.1, s32[2]{0:T(128)} %len_ref.1, bf16[2,128,1024]{2,1,0:T(8,128)(2,1)} %x_hbm.1, bf16[2,2,64]{2,1,0:T(2,128)(2,1)} %lna_hbm.1, bf16[2,2,64]{2,1,0:T(2,128)(2,1)} %lnm_hbm.1, ...), custom_call_target="tpu_custom_call" | custom-call | tf_op jit(solution)/shard_map/pallas_call | solution.py:467
  159.5 0.0 copy-start.1
  159.5 2.0 %copy.15 = bf16[2,128,1024]{2,1,0:T(8,128)(2,1)} copy(bf16[2,128,1024]{2,1,0:T(8,128)(2,1)} %get-tuple-element.12) | data formatting | bytes 1048576
  161.4 0.0 copy-done.1
  161.4 0.0 copy-start
  161.4 1.0 copy.16
  162.4 0.6 copy-done
  163.0 1.0 copy.17
Async XLA Ops:
  159.5 2.0 %copy-start.1 = (bf16[2,2,16,64,128]{4,3,2,1,0:T(8,128)(2,1)S(1)}, bf16[2,2,16,64,128]{4,3,2,1,0:T(8,128)(2,1)}, u32[]{:S(2)}) copy-start(bf16[2,2,16,64,128]{4,3,2,1,0:T(8,128)(2,1)} %get-tuple-element.7) | copy-start | bytes 3145732
  161.4 1.6 copy-start

commit v4 on v2

--- a/solution.py
+++ b/solution.py
@@ -1,4 +1,5 @@
 import functools
+import heapq
 import math
 
 import jax
@@ -14,7 +15,9 @@
 F32 = jnp.float32
 BF16 = jnp.bfloat16
 QUARTERS = 4
-UNITS = 3
+MODEL = (46.6e3, 300e3, 3.0, 1.5, 2.0, 6.0, 3.0, 0.05)
+WORK_US = (1.9, 0.5, 0.7, 0.5, 0.5)
+UNITS = 5
 
 
 def kernel(
@@ -34,8 +37,10 @@
     k_hbm,
     v_hbm,
     buf_q,
-    buf_u,
-    buf_d,
+    buf_u0,
+    buf_u1,
+    buf_d0,
+    buf_d1,
     up_nat,
     out_nat,
     x_nat,
@@ -45,6 +50,8 @@
     ctx_t,
     hid_t,
     acc,
+    mlp,
+    y_nat,
     ln_all,
     ln_own,
     ln_nat,
@@ -63,8 +70,10 @@
     ln_sib,
     load_sem,
     cache_sem,
+    y_sem,
 ):
     half = chips // 2
+    seq = x_hbm.shape[1]
     d_me = lax.axis_index("dp")
     w_me = lax.axis_index("wg")
     z, c = w_me // 2, w_me % 2
@@ -75,7 +84,7 @@
     dev_sib = {"wg": z * 2 + 1 - c}
     quarter_z = (px, 2 + py)
     quarter_xy = (1 - px, 3 - py)
-    bufs = (buf_q, buf_u, buf_d)
+    bufs = (buf_q, buf_u0, buf_u1, buf_d0, buf_d1)
     hops = ((half, half - 1), (half - 1, half))
 
     def chip_at(direction, h):
@@ -115,23 +124,19 @@
     def send_own_sib(l, u):
         sib_copy(l, u, z, c, chips - 1).start()
 
-    def forward(l, u, h, s):
-        for direction in (0, 1):
-            if h > hops[direction][s]:
-                continue
-            z_arrival(l, u, direction, s, h).wait_recv()
-            if h < hops[direction][s]:
-                z_copy(l, u, direction, s, h + 1).start()
-            xy_copy(l, u, direction, s, h, quarter_z[s]).start()
+    def land(l, u, direction, s, h):
+        z_arrival(l, u, direction, s, h).wait_recv()
+        if h < hops[direction][s]:
+            z_copy(l, u, direction, s, h + 1).start()
+        xy_copy(l, u, direction, s, h, quarter_z[s]).start()
 
     def sources(h):
         return (0, 1) if h < half else (0,)
 
-    def share_with_sibling(l, u, h):
-        for direction in sources(h):
-            for s in (0, 1):
-                xy_copy(l, u, direction, s, h, quarter_xy[s]).wait_recv()
-            sib_copy(l, u, chip_at(direction, h), c, source_index(direction, h)).start()
+    def share_with_sibling(l, u, direction, h):
+        for s in (0, 1):
+            xy_copy(l, u, direction, s, h, quarter_xy[s]).wait_recv()
+        sib_copy(l, u, chip_at(direction, h), c, source_index(direction, h)).start()
 
     def wait_sibling(l, u, h):
         for direction in sources(h):
@@ -154,6 +159,11 @@
 
     def ln_share(core):
         return remote(ln_all.at[core], ln_all.at[core], ln_sib.at[0], ln_sib.at[1], dev_sib)
+
+    def y_copy(chip):
+        columns = y_nat.shape[3]
+        dst = y_hbm.at[:, :, pl.ds(pl.multiple_of(chip * columns, columns), columns)]
+        return pltpu.make_async_copy(y_nat.at[chip], dst, y_sem.at[chip])
 
 
     def normalize(l):
@@ -180,57 +190,81 @@
         cos, sin = cos_ref[...], sin_ref[...]
         k_index = lax.broadcasted_iota(jnp.int32, (seq, seq), 0)
         q_index = lax.broadcasted_iota(jnp.int32, (seq, seq), 1)
+        chains = [(core, b) for core in (0, 1) for b in range(k_ref.shape[1])]
+        qkvs, q_ts, k_ts, all_scores, probs = {}, {}, {}, {}, {}
         for core in (0, 1):
-            head = chip * 2 + core
             share = buf_q[l, pl.ds(slot(chip, core, 0), QUARTERS)]
             share = share.reshape(-1, share.shape[-1])
-            qkv = jnp.dot(share, a_t[...], preferred_element_type=F32).astype(BF16)
-            for b in range(k_ref.shape[1]):
-                cols_b = slice(b * seq, (b + 1) * seq)
-                q_t = rotate(qkv[:head_dim, cols_b], cos, sin)
-                k_t = rotate(qkv[head_dim : 2 * head_dim, cols_b], cos, sin)
-                v_t = qkv[2 * head_dim :, cols_b]
-                k_ref[l, b, head] = k_t
-                v_ref[l, b, head] = v_t
-                scores = jnp.dot(k_t.T, q_t, preferred_element_type=F32) * head_dim**-0.5
-                allowed = (k_index <= q_index) & (k_index < len_ref[b])
-                scores = jnp.where(allowed, scores, -1e30)
-                top = jnp.max(scores, axis=0, keepdims=True)
-                expo = jnp.exp(scores - top)
-                prob = (expo * (1.0 / jnp.sum(expo, axis=0, keepdims=True))).astype(BF16)
-                ctx_t[head, :, cols_b] = jnp.dot(v_t, prob, preferred_element_type=F32).astype(BF16)
-
-    def compute_up(l, chip):
-        up_rows = up_hbm.shape[2] // QUARTERS
-        for core in (0, 1):
-            share = buf_u[l, pl.ds(slot(chip, core, 0), QUARTERS), :up_rows, :]
-            share = share.reshape(-1, share.shape[-1])
-            pre = jnp.dot(share, m_t[...], preferred_element_type=F32)
-            hid_t[chip * 2 + core] = (0.5 * pre * (1.0 + lax.erf(pre * 0.5**0.5))).astype(BF16)
-        share = buf_u[l, pl.ds(slot(chip, 0, 0), 2 * QUARTERS), up_rows:, :]
+            qkvs[core] = jnp.dot(share, a_t[...], preferred_element_type=F32).astype(BF16)
+        for core, b in chains:
+            cols_b = slice(b * seq, (b + 1) * seq)
+            qkv = qkvs[core]
+            q_ts[core, b] = rotate(qkv[:head_dim, cols_b], cos, sin)
+            k_ts[core, b] = rotate(qkv[head_dim : 2 * head_dim, cols_b], cos, sin)
+            k_ref[l, b, chip * 2 + core] = k_ts[core, b]
+            v_ref[l, b, chip * 2 + core] = qkv[2 * head_dim :, cols_b]
+        for chain in chains:
+            all_scores[chain] = jnp.dot(k_ts[chain].T, q_ts[chain], preferred_element_type=F32)
+        for core, b in chains:
+            scores = all_scores[core, b] * head_dim**-0.5
+            allowed = (k_index <= q_index) & (k_index < len_ref[b])
+            scores = jnp.where(allowed, scores, -1e30)
+            top = jnp.max(scores, axis=0, keepdims=True)
+            expo = jnp.exp(scores - top)
+            probs[core, b] = (expo * (1.0 / jnp.sum(expo, axis=0, keepdims=True))).astype(BF16)
+        for core, b in chains:
+            cols_b = slice(b * seq, (b + 1) * seq)
+            v_t = qkvs[core][2 * head_dim :, cols_b]
+            ctx_t[chip * 2 + core, :, cols_b] = jnp.dot(v_t, probs[core, b], preferred_element_type=F32).astype(BF16)
+
+    def up_half(i, share, chip):
+        rows = hid_t.shape[1] // 2
+        pre = jnp.dot(share.reshape(-1, share.shape[-1]), m_t[...], preferred_element_type=F32)
+        hidden = (0.5 * pre * (1.0 + lax.erf(pre * 0.5**0.5))).astype(BF16)
+        hid_t[pl.ds(chip * 2, 2), i * rows : (i + 1) * rows, :] = hidden.reshape(2, rows, hidden.shape[-1])
+
+    def compute_up_0(l, chip):
+        up_half(0, buf_u0[l, pl.ds(slot(chip, 0, 0), 2 * QUARTERS)], chip)
+
+    def compute_up_1(l, chip):
+        both = pl.ds(slot(chip, 0, 0), 2 * QUARTERS)
+        rows = buf_u0.shape[2]
+        up_half(1, buf_u1[l, both, :rows, :], chip)
+        share = buf_u1[l, both, rows:, :]
         share = share.reshape(-1, share.shape[-1])
         ctx = ctx_t[...].reshape(-1, ctx_t.shape[-1])
         attn_out = jnp.dot(share, ctx, preferred_element_type=F32)
         acc[pl.ds(chip * 2, 2)] = attn_out.reshape((2,) + acc.shape[1:])
 
-    def compute_down(l, chip):
-        share = buf_d[l, pl.ds(slot(chip, 0, 0), 2 * QUARTERS)]
+    def down_half(buf, i, l, chip):
+        share = buf[l, pl.ds(slot(chip, 0, 0), 2 * QUARTERS)]
         share = share.reshape(-1, share.shape[-1])
-        hidden = hid_t[...].reshape(-1, hid_t.shape[-1])
-        mlp_out = jnp.dot(share, hidden, preferred_element_type=F32).reshape((2,) + acc.shape[1:])
+        hidden = hid_t[i * chips : (i + 1) * chips].reshape(-1, hid_t.shape[-1])
+        return jnp.dot(share, hidden, preferred_element_type=F32).reshape((2,) + acc.shape[1:])
+
+    def compute_down_0(l, chip):
+        mlp[pl.ds(chip * 2, 2)] = down_half(buf_d0, 0, l, chip)
+
+    def compute_down_1(l, chip):
         both = pl.ds(chip * 2, 2)
-        x_t[both] = (x_t[both].astype(F32) + acc[both] + mlp_out).astype(BF16)
-
-    computes = (compute_qkv, compute_up, compute_down)
+        mlp_out = mlp[both] + down_half(buf_d1, 1, l, chip)
+        rows = (x_t[both].astype(F32) + acc[both] + mlp_out).astype(BF16)
+        x_t[both] = rows
+
+        if l == layers - 1:
+            block = rows.reshape(-1, rows.shape[-1])
+            for b in range(x_nat.shape[0]):
+                y_nat[chip, b] = block[:, b * seq : (b + 1) * seq].T
+            y_copy(chip).start()
+
+    computes = (compute_qkv, compute_up_0, compute_up_1, compute_down_0, compute_down_1)
 
     def compute(l, u, h):
         wait_sibling(l, u, h)
         if u == 0 and h == 1:
 
-            @pl.when(l == 0)
-            def _():
+            if l == 0:
                 ln_share(1 - c).wait_recv()
-
             normalize(l)
 
         @pl.loop(0, 2)
@@ -241,11 +275,16 @@
 
     own = pl.ds(slot(z, c, 0), QUARTERS)
     loads = [pltpu.make_async_copy(qkv_hbm.at[l], buf_q.at[l, own], load_sem.at[l]) for l in range(layers)]
-    loads += [pltpu.make_async_copy(down_hbm.at[l], buf_d.at[l, own], load_sem.at[layers + l]) for l in range(layers)]
-    load_up = pltpu.make_async_copy(up_hbm, up_nat, load_sem.at[2 * layers])
-    load_out = pltpu.make_async_copy(out_hbm, out_nat, load_sem.at[2 * layers + 1])
-    load_x = pltpu.make_async_copy(x_hbm, x_nat, load_sem.at[2 * layers + 2])
-    load_ln = [pltpu.make_async_copy(src, ln_nat.at[i], load_sem.at[2 * layers + 3 + i]) for i, src in enumerate((lna_hbm, lnm_hbm))]
+    width = buf_d0.shape[3]
+    loads += [
+        pltpu.make_async_copy(down_hbm.at[l, :, :, i * width : (i + 1) * width], dst.at[l, own], load_sem.at[(1 + i) * layers + l])
+        for i, dst in enumerate((buf_d0, buf_d1))
+        for l in range(layers)
+    ]
+    load_up = pltpu.make_async_copy(up_hbm, up_nat, load_sem.at[3 * layers + 0])
+    load_out = pltpu.make_async_copy(out_hbm, out_nat, load_sem.at[3 * layers + 1])
+    load_x = pltpu.make_async_copy(x_hbm, x_nat, load_sem.at[3 * layers + 2])
+    load_ln = [pltpu.make_async_copy(src, ln_nat.at[i], load_sem.at[3 * layers + 3 + i]) for i, src in enumerate((lna_hbm, lnm_hbm))]
     for load in [loads[0]] + load_ln + [load_x, load_up, load_out] + loads[1:]:
         load.start()
 
@@ -266,8 +305,19 @@
     send_own(0, 0, 1)
     ln_hop(0)
     send_own_sib(0, 0)
+    load_up.wait()
+    load_out.wait()
+    def place_up(l):
+        up_t = up_nat[l].T
+        out_t = out_nat[l].T
+        rows = up_t.shape[0] // 2
+        half_rows = buf_u0.shape[2]
+        buf_u0[l, own] = up_t[:rows].reshape(QUARTERS, half_rows, -1)
+        buf_u1[l, own, :half_rows, :] = up_t[rows:].reshape(QUARTERS, half_rows, -1)
+        buf_u1[l, own, half_rows:, :] = out_t.reshape(QUARTERS, -1, out_t.shape[-1])
+
+    place_up(0)
     load_x.wait()
-    seq = x_hbm.shape[1]
     for b in range(x_hbm.shape[0]):
         x_t[:, :, b * seq : (b + 1) * seq] = x_nat[b].T.reshape(x_t.shape[0], x_t.shape[1], seq)
     half_dim = cos_ref.shape[0]
@@ -276,42 +326,8 @@
     angles = position * ROPE_BASE ** (-row * 2.0 / (2 * half_dim))
     cos_ref[...] = jnp.cos(angles)
     sin_ref[...] = jnp.sin(angles)
-    load_up.wait()
-    load_out.wait()
-    up_rows = up_hbm.shape[2] // QUARTERS
-
-    def place_up(l):
-        up_t = up_nat[l].T
-        buf_u[l, own, :up_rows, :] = up_t.reshape(QUARTERS, up_rows, up_t.shape[-1])
-        out_t = out_nat[l].T
-        buf_u[l, own, up_rows:, :] = out_t.reshape(QUARTERS, -1, out_t.shape[-1])
-
-    place_up(0)
     ln_hop(1)
 
-
-    period = 2 * UNITS
-    lands, shares, works = ([[] for _ in range(period)] for _ in range(3))
-    for h in range(1, half + 1):
-        for u in range(UNITS):
-            landing = 2 * u + h
-            work = 2 * u + half + (h > half // 2)
-            for table, n in ((lands, landing), (shares, landing + 1), (works, work)):
-                table[n % period].append((u, h, n // period))
-
-    def run(action, table, l):
-        for late in (0, 1):
-            items = [(u, h) for u, h, lateness in table if lateness == late]
-            if items:
-
-                @pl.when(l < layers if late == 0 else l > 0)
-                def _():
-                    for u, h in items:
-                        action(l - late, u, h)
-
-    def land(l, u, h):
-        forward(l, u, h, 0)
-        forward(l, u, h, 1)
 
     def work(l, u, h):
         compute(l, u, h)
@@ -325,40 +341,34 @@
             for i, (src, dst) in enumerate(((k_ref, k_hbm), (v_ref, v_hbm)))
         ]
 
-    @pl.loop(0, layers + 1)
-    def _(l):
-        for n in range(period):
-            if n % 2 == 0:
-                u = n // 2
-
-                @pl.when((l < layers) & (l + u > 0))
-                def _():
-                    for s in (0, 1):
-                        send_own(l, u, s)
-                    send_own_sib(l, u)
-
-            run(land, lands[n], l)
-            if n in (1, 2, 3):
-
-                @pl.when(l == 0)
-                def _():
-                    ln_hop(n + 1)
-                    if n == 2:
-                        for load in loads[1:]:
-                            load.wait()
-                        for later in range(1, layers):
-                            place_up(later)
-                    if n == 3:
+    sizes = [math.prod(ref.shape[2:]) * 2 for ref in bufs] * layers
+    plan = travel_plan(sizes, WORK_US * layers, half)
+    seen = [0] * (half + 1)
+    for action, n, *where in plan:
+        l, u = n // UNITS, n % UNITS
+        if action == "own":
+            if n == 3:
+                for load in loads[1:]:
+                    load.wait()
+                for later in range(1, layers):
+                    place_up(later)
+            if n > 0:
+                send_own(l, u, 0)
+                send_own(l, u, 1)
+                send_own_sib(l, u)
+        elif action == "z":
+            land(l, u, *where)
+            h = where[-1]
+            if n == 0 and h < half:
+                seen[h] += 1
+                if seen[h] == 4:
+                    ln_hop(h + 1)
+                    if h + 1 == half:
                         ln_share(c).start()
-
-            run(share_with_sibling, shares[n], l)
-            run(work, works[n], l)
-
-    y_t = x_t[...].reshape(-1, x_t.shape[-1])
-    for b in range(x_hbm.shape[0]):
-        x_nat[b] = y_t[:, b * seq : (b + 1) * seq].T
-    store_y = pltpu.make_async_copy(x_nat, y_hbm, load_sem.at[2 * layers + 2])
-    store_y.start()
+        elif action == "give":
+            share_with_sibling(l, u, *where)
+        else:
+            work(l, u, *where)
 
     ref = ln_all.at[c]
     for direction in (0, 1):
@@ -378,7 +388,107 @@
         for copy in cache_copies(l):
             copy.wait()
 
-    store_y.wait()
+
+    @pl.loop(0, chips)
+    def _(chip):
+        y_copy(chip).wait()
+
+
+def travel_plan(sizes, work_us, half):
+    link_rate, core_rate, hop_us, core_us, slack, depth, start_us, issue_us = MODEL
+    hops = ((half, half - 1), (half - 1, half))
+    queue = dict.fromkeys((0, 1, "x", "y", "core"), 0.0)
+    events, plan, parts, shared = [], [], {}, set()
+    now, started = 0.0, 0
+    works = [(u, h) for u in range(len(sizes)) for h in range(1, half + 1)]
+    ln_left, ln_time = 4, None
+
+    def send(link, size, tag):
+        queue[link] = max(now, queue[link]) + size / (core_rate if link == "core" else link_rate)
+        late = 0.0 if tag[0] == "z" else slack
+        heapq.heappush(events, (queue[link] + (core_us if link == "core" else hop_us) + late, len(events) + len(plan) * 1000, tag))
+
+    def source(direction, h):
+        return (direction, h) if h < half else (0, half)
+
+    def ready(u, h):
+        needs = [(u,) + source(direction, h) for direction in ((0, 1) if h < half else (0,))]
+        needs += [(u, 0, 0)] if h == half else []
+        return ln_time is not None and now >= ln_time and all(need in shared for need in needs)
+
+    while True:
+        while started < len(sizes) and min(queue[0], queue[1]) - now < depth:
+            plan.append(("own", started))
+            for s in (0, 1):
+                for direction in (0, 1):
+                    send(direction, sizes[started], ("z", started, direction, s, 1))
+            send("core", 4 * sizes[started], ("core", started, 0, 0))
+            started += 1
+            if started == 1:
+                now += start_us
+        can_work = bool(works) and ready(*works[0])
+        if events and (events[0][0] <= now or not can_work):
+            at, _, tag = heapq.heappop(events)
+            now = max(now, at) + issue_us
+            if tag[0] == "core":
+                shared.add(tag[1:])
+                continue
+            _, u, direction, s, h = tag
+            if tag[0] == "z":
+                plan.append(tag)
+                if h < hops[direction][s]:
+                    send(direction, sizes[u], ("z", u, direction, s, h + 1))
+                send("xy"[s], sizes[u], ("xy", u, direction, s, h))
+                if u == 0 and h == half - 1:
+                    ln_left -= 1
+                    ln_time = now + 2 * hop_us if ln_left == 0 else None
+            key = (u,) + source(direction, h)
+            parts[key] = parts.get(key, 0) + 1
+            if parts[key] == 4:
+                plan.append(("give",) + key)
+                send("core", 4 * sizes[u], ("core",) + key)
+        elif works:
+            if not can_work:
+                now = max(now, ln_time)
+                continue
+            u, h = works.pop(0)
+            plan.append(("work", u, h))
+            now += work_us[u]
+        else:
+            return plan
+
+
+def settle_kernel(*refs):
+    count = (len(refs) - 2) // 3
+    arrays, results, held = refs[:count], refs[count : 2 * count], refs[2 * count : 3 * count]
+    read_sem, write_sem = refs[3 * count :]
+    parts = [(i, p) for p in range(arrays[0].shape[0]) for i in range(count)]
+
+    def read(i, p):
+        return pltpu.make_async_copy(arrays[i].at[p], held[i].at[p], read_sem.at[i, p])
+
+    def write(i, p):
+        return pltpu.make_async_copy(held[i].at[p], results[i].at[p], write_sem.at[i, p])
+
+    for i, p in parts:
+        read(i, p).start()
+    for i, p in parts:
+        read(i, p).wait()
+        write(i, p).start()
+    for i, p in parts:
+        write(i, p).wait()
+
+
+def settle(*arrays):
+    any_spec = pl.BlockSpec(memory_space=pl.ANY)
+    sem = pltpu.SemaphoreType.DMA((len(arrays), arrays[0].shape[0]))
+    return pl.pallas_call(
+        settle_kernel,
+        out_shape=tuple(jax.ShapeDtypeStruct(a.shape, a.dtype) for a in arrays),
+        in_specs=[any_spec] * len(arrays),
+        out_specs=(any_spec,) * len(arrays),
+        scratch_shapes=[pltpu.VMEM(a.shape, a.dtype) for a in arrays] + [sem, sem],
+    )(*arrays)
 
 
 def solution(mesh):
@@ -411,8 +521,10 @@
             out_specs=(any_spec,) * 3,
             scratch_shapes=[
                 pltpu.VMEM((layers, slots) + qkv_t.shape[2:], BF16),
-                pltpu.VMEM((layers, slots, up_rows + out_rows, width), BF16),
-                pltpu.VMEM((layers, slots) + down_t.shape[2:], BF16),
+                pltpu.VMEM((layers, slots, up_rows // 2, width), BF16),
+                pltpu.VMEM((layers, slots, up_rows // 2 + out_rows, width), BF16),
+                pltpu.VMEM((layers, slots, down_t.shape[2], down_t.shape[3] // 2), BF16),
+                pltpu.VMEM((layers, slots, down_t.shape[2], down_t.shape[3] // 2), BF16),
                 pltpu.VMEM(w_up.shape, BF16),
                 pltpu.VMEM(out_nat.shape, BF16),
                 pltpu.VMEM(x.shape, BF16),
@@ -422,6 +534,8 @@
                 pltpu.VMEM((heads, head_dim, tokens), BF16),
                 pltpu.VMEM((shares, w_up.shape[2], tokens), BF16),
                 pltpu.VMEM((shares, width // shares, tokens), F32),
+                pltpu.VMEM((shares, width // shares, tokens), F32),
+                pltpu.VMEM((chips, prompts, seq, width // chips), BF16),
                 pltpu.VMEM((2, chips, layers, 8, 128), F32),
                 pltpu.VMEM((layers, 8, 128), F32),
                 pltpu.VMEM((2,) + ln_attn.shape, BF16),
@@ -438,13 +552,15 @@
                 dma((2, chips // 2)),
                 dma((2,)),
                 dma((2,)),
-                dma((2 * layers + 5,)),
+                dma((3 * layers + 5,)),
                 dma((layers, 2)),
+                dma((chips,)),
             ],
             compiler_params=pltpu.CompilerParams(
                 collective_id=0, has_side_effects=True, vmem_limit_bytes=67043328
             ),
         )(positions, prompt_len, x, ln_attn, ln_mlp, qkv_t, w_up, out_nat, down_t)
+        y, k_cache, v_cache = settle(y, k_cache, v_cache)
         order = (0, 1, 4, 2, 3)
         return y, k_cache.transpose(order), v_cache.transpose(order)
 

time: 156 us -> 151 us (0.968)
  local copies, waits for them, and re-layouts: 4.53 us -> 0 us
    unnamed x7 -> x0, local copies, waits for them, and re-layouts: 4.53 us -> none
    pallas_call x1, Pallas kernels: 151 us -> 147 us  [local_program(): pl.pallas_call(functools.partial(kernel, cols, chips, layers), out_shape=...]
    pallas_call x0 -> x1, Pallas kernels: none -> 2.63 us  [settle(): pl.pallas_call(settle_kernel, out_shape=tuple((jax.ShapeDtypeStruct(a.sha...]
where the time goes in v4:
time: 151 us
  Pallas kernels  150 us (99%)
    pallas_call x1, Pallas kernels, local_program(): pl.pallas_call(functools.partial(kernel, cols, chips, layers), out_shape=...  147 us

profile of v4, /device:TPU:21, one launch (start us, length us, event | category | flops | bytes accessed | tf_op | source)
XLA Modules:
  0.0 150.7 jit_solution(3519919984869727003)
XLA Ops:
  0.6 147.3 %shard_map.112 = (bf16[2,128,1024]{2,1,0:T(8,128)(2,1)}, bf16[2,2,16,64,128]{4,3,2,1,0:T(8,128)(2,1)}, bf16[2,2,16,64,128]{4,3,2,1,0:T(8,128)(2,1)}) custom-call(s32[128]{0:T(128)} %pos_ref.1, s32[2]{0:T(128)} %len_ref.1, bf16[2,128,1024]{2,1,0:T(8,128)(2,1)} %x_hbm.1, bf16[2,2,64]{2,1,0:T(2,128)(2,1)} %lna_hbm.1, bf16[2,2,64]{2,1,0:T(2,128)(2,1)} %lnm_hbm.1, ...), custom_call_target="tpu_custom_call" | custom-call | tf_op jit(solution)/shard_map/pallas_call | solution.py:517
  147.9 2.6 %shard_map.113 = (bf16[2,128,1024]{2,1,0:T(8,128)(2,1)}, bf16[2,2,16,64,128]{4,3,2,1,0:T(8,128)(2,1)}, bf16[2,2,16,64,128]{4,3,2,1,0:T(8,128)(2,1)}) custom-call(bf16[2,128,1024]{2,1,0:T(8,128)(2,1)} %get-tuple-element.9.refs_0_, bf16[2,2,16,64,128]{4,3,2,1,0:T(8,128)(2,1)} %get-tuple-element.10.refs_1_, bf16[2,2,16,64,128]{4,3,2,1,0:T(8,128)(2,1)} %get-tuple-element.11.refs_2_), custom_call_target="tpu_custom_call" | custom-call | tf_op jit(solution)/shard_map/pallas_call | solution.py:485

commit v5 on v4

--- a/solution.py
+++ b/solution.py
@@ -15,7 +15,7 @@
 F32 = jnp.float32
 BF16 = jnp.bfloat16
 QUARTERS = 4
-MODEL = (46.6e3, 300e3, 3.0, 1.5, 2.0, 6.0, 3.0, 0.05)
+MODEL = (46.6e3, 300e3, 2.8, 1.5, 2.0, 1.0, 3.5, 0.03)
 WORK_US = (1.9, 0.5, 0.7, 0.5, 0.5)
 UNITS = 5
 
@@ -292,19 +292,18 @@
     neighbours = dev_z + dev_xy + (dev_sib,)
     for dev in neighbours:
         pl.semaphore_signal(barrier, inc=1, device_id=dev, device_id_type=MESH)
+    loads[0].wait()
+    pl.semaphore_wait(barrier, len(neighbours))
+
+    send_own(0, 0, 0)
+    send_own(0, 0, 1)
+    send_own_sib(0, 0)
     ln_own[...] = jnp.zeros_like(ln_own)
     for i in (0, 1):
         load_ln[i].wait()
         for l in range(layers):
             ln_own[l, 2 * i : 2 * i + 2, : ln_nat.shape[3]] = ln_nat[i, l].astype(F32)
     ln_all[c, z] = ln_own[...]
-    loads[0].wait()
-    pl.semaphore_wait(barrier, len(neighbours))
-
-    send_own(0, 0, 0)
-    send_own(0, 0, 1)
-    ln_hop(0)
-    send_own_sib(0, 0)
     load_up.wait()
     load_out.wait()
     def place_up(l):
@@ -317,6 +316,7 @@
         buf_u1[l, own, half_rows:, :] = out_t.reshape(QUARTERS, -1, out_t.shape[-1])
 
     place_up(0)
+    ln_hop(0)
     load_x.wait()
     for b in range(x_hbm.shape[0]):
         x_t[:, :, b * seq : (b + 1) * seq] = x_nat[b].T.reshape(x_t.shape[0], x_t.shape[1], seq)

time: 151 us -> 150 us (level)
  no operation moved by 1% of the time
where the time goes in v5:
time: 150 us
  Pallas kernels  149 us (99%)
    pallas_call x1, Pallas kernels, local_program(): pl.pallas_call(functools.partial(kernel, cols, chips, layers), out_shape=...  147 us

profile of v5, /device:TPU:21, one launch (start us, length us, event | category | flops | bytes accessed | tf_op | source)
XLA Modules:
  0.0 150.1 jit_solution(9162774579737941445)
XLA Ops:
  0.6 146.6 %shard_map.112 = (bf16[2,128,1024]{2,1,0:T(8,128)(2,1)}, bf16[2,2,16,64,128]{4,3,2,1,0:T(8,128)(2,1)}, bf16[2,2,16,64,128]{4,3,2,1,0:T(8,128)(2,1)}) custom-call(s32[128]{0:T(128)} %pos_ref.1, s32[2]{0:T(128)} %len_ref.1, bf16[2,128,1024]{2,1,0:T(8,128)(2,1)} %x_hbm.1, bf16[2,2,64]{2,1,0:T(2,128)(2,1)} %lna_hbm.1, bf16[2,2,64]{2,1,0:T(2,128)(2,1)} %lnm_hbm.1, ...), custom_call_target="tpu_custom_call" | custom-call | tf_op jit(solution)/shard_map/pallas_call | solution.py:517
  147.3 2.6 %shard_map.113 = (bf16[2,128,1024]{2,1,0:T(8,128)(2,1)}, bf16[2,2,16,64,128]{4,3,2,1,0:T(8,128)(2,1)}, bf16[2,2,16,64,128]{4,3,2,1,0:T(8,128)(2,1)}) custom-call(bf16[2,128,1024]{2,1,0:T(8,128)(2,1)} %get-tuple-element.9.refs_0_, bf16[2,2,16,64,128]{4,3,2,1,0:T(8,128)(2,1)} %get-tuple-element.10.refs_1_, bf16[2,2,16,64,128]{4,3,2,1,0:T(8,128)(2,1)} %get-tuple-element.11.refs_2_), custom_call_target="tpu_custom_call" | custom-call | tf_op jit(solution)/shard_map/pallas_call | solution.py:485
